TPU v7x, 32 devices: a whole 2x2x4 slice. The times are simulated.
32 devices in a mesh: gx: 4 (over y, core), gy: 8 (over z, x).
Axes of the slice: x: 2, y: 2, z: 4, core: 2. Of those that a mesh axis runs over, the one named last changes fastest.
Arguments:
- radiation: float32 [2, 4, 8, 64, 1024], P(None, None, None, 'gx', 'gy'), may hold values from -4 to 4, as said below
- ion_fraction: float32 [8, 64, 1024], P(None, 'gx', 'gy'), may hold values from 0.05 to 0.95
- density: float32 [8, 64, 1024], P(None, 'gx', 'gy'), may hold values from 0.1 to 10
- star_lum: float32 [4, 8, 2, 256], P('gx', 'gy'), may hold values from 0.1 to 10
- star_cell: int32 [4, 8, 3, 256], P('gx', 'gy'), may hold values from 0 to 127, as said below
- star_offset: float32 [4, 8, 3, 256], P('gx', 'gy'), may hold values from 0 to 1
- star_count: int32 [4, 8], P('gx', 'gy'), may hold values from 1 to 256, as said below
Outputs:
- radiation_out: float32 [2, 4, 8, 64, 1024], P(None, None, None, 'gx', 'gy')
- ion_out: float32 [8, 64, 1024], P(None, 'gx', 'gy')
Inputs may be any that keep to these rules, and one draw needn't show every extreme that they name: `star_cell`: per slot: row 0 is the x corner within the tile, 0 to 15; row 1 the y corner, 0 to 127; row 2 the z corner, 0 to 7. `star_count`: some tile has all 256 slots live in every draw. `radiation`: N is positive and |F| < N in every cell.
All inputs are finite; a program needn't handle non-finite values.
Results may differ from a plain program's by a relative error of at most 0.0001.
Values sent between devices are 32-bit elements; how exact they have to be, the bound alone decides.
No kernel may reach another device: no remote copies, remote signals or barrier semaphores. Data moves between devices by JAX's collectives and lax.ppermute only.
A program may use at most 64 MiB of HBM per device.

v0:
```python
import jax
import jax.numpy as jnp
from jax import lax
from jax.sharding import PartitionSpec as P

SUBSTEPS = 4
CHEM_ITERS = 3


DT = 0.3
ALPHA = 0.4
SIGMA = (1.5, 0.5)


def shifted(value, axis, steps):
    count = lax.axis_size(axis)
    pairs = [(source, (source + steps) % count) for source in range(count)]
    return lax.ppermute(value, axis, pairs)


def padded_2(block, sides, width):
    for axis, dim in sides:
        count = lax.axis_size(axis)
        forward = [(i, i + 1) for i in range(count - 1)]
        forward.append((count - 1, 0))
        backward = [(target, source) for source, target in forward]
        low = lax.ppermute(
            lax.slice_in_dim(block, block.shape[dim] - width, None, axis=dim), axis, forward
        )
        high = lax.ppermute(lax.slice_in_dim(block, 0, width, axis=dim), axis, backward)
        block = jnp.concatenate([low, block, high], axis=dim)
    return block


def directional(state, axis_dir):
    photons = state[:, 0]
    flux = state[:, 1:4]
    fsq = jnp.minimum(jnp.sum(flux * flux, axis=1) / (photons * photons), 1.0)
    root = jnp.sqrt(4.0 - 3.0 * fsq)
    chi = (3.0 + 4.0 * fsq) / (5.0 + 2.0 * root)
    shape_term = (3.0 / (2.0 + root) + 6.0) / (5.0 + 2.0 * root)
    diag = 0.5 * (1.0 - chi) * photons
    scaled = shape_term / photons
    comps = [flux[:, axis_dir]]
    for other in range(3):
        value = scaled * flux[:, axis_dir] * flux[:, other]
        if other == axis_dir:
            value = value + diag
        comps.append(value)
    return jnp.stack(comps, axis=1)


def transport(padded):
    phys_z = directional(padded, 2)
    face_z = 0.5 * (phys_z + jnp.roll(phys_z, -1, 2)) - 0.5 * (jnp.roll(padded, -1, 2) - padded)
    div_z = (face_z - jnp.roll(face_z, 1, 2))[..., 1:-1, 1:-1]
    phys_x = directional(padded, 0)
    face_x = 0.5 * (phys_x[..., :-1, :] + phys_x[..., 1:, :]) - 0.5 * (
        padded[..., 1:, :] - padded[..., :-1, :]
    )
    div_x = (face_x[..., 1:, :] - face_x[..., :-1, :])[..., 1:-1]
    phys_y = directional(padded, 1)
    face_y = 0.5 * (phys_y[..., :-1] + phys_y[..., 1:]) - 0.5 * (padded[..., 1:] - padded[..., :-1])
    div_y = (face_y[..., 1:] - face_y[..., :-1])[..., 1:-1, :]
    return padded[..., 1:-1, 1:-1] - DT * (div_x + div_y + div_z)


def chemistry(state, ion, dens):
    sig = jnp.array(SIGMA, jnp.float32).reshape(2, 1, 1, 1)
    start_n = state[:, 0]
    start_f = state[:, 1:4]
    frac = ion
    for step in range(CHEM_ITERS):
        atten = 1.0 / (1.0 + DT * sig * dens * (1.0 - frac))
        photons = start_n * atten
        gamma = jnp.sum(sig * photons, axis=0)
        frac = (ion + DT * gamma) / (1.0 + DT * (gamma + ALPHA * dens * frac))
    return (jnp.concatenate([photons[:, None], start_f * atten[:, None]], axis=1), frac)


def add_source(state, emission):
    return jnp.concatenate([state[:, :1] + DT * emission[:, None], state[:, 1:]], axis=1)


def corner_weights(coord, frac, width, wrapped):
    cells = jnp.arange(width, dtype=jnp.int32)[None, :]
    upper = (coord + 1) % width if wrapped else coord + 1
    lower_hit = (coord[:, None] == cells).astype(jnp.float32)
    upper_hit = (upper[:, None] == cells).astype(jnp.float32)
    return lower_hit * (1.0 - frac)[:, None] + upper_hit * frac[:, None]


def on_device(radiation, ion_fraction, density, star_lum, star_cell, star_offset, star_count):
    groups, comps, depth, rows_x, rows_y = radiation.shape
    slots = star_lum.shape[3]
    live = (jnp.arange(slots, dtype=jnp.int32) < star_count[0, 0]).astype(jnp.float32)
    cells = star_cell[0, 0]
    offsets = star_offset[0, 0]
    weight_z = corner_weights(cells[2], offsets[2], depth, True)
    weight_x = corner_weights(cells[0], offsets[0], rows_x + 1, False)
    weight_y = corner_weights(cells[1], offsets[1], rows_y + 1, False)
    strength = star_lum[0, 0] * live[None, :]
    spread = strength[:, :, None, None] * weight_z[None, :, :, None] * weight_x[None, :, None, :]
    spread = spread.transpose(0, 2, 3, 1).reshape(-1, slots)
    extended = jnp.dot(
        spread, weight_y, precision=lax.Precision.HIGHEST, preferred_element_type=jnp.float32
    )
    extended = extended.reshape(groups, depth, rows_x + 1, rows_y + 1)
    incoming_x = shifted(extended[:, :, rows_x:, :], "gx", 1)
    owned_x = extended[:, :, :rows_x, :]
    owned_x = jnp.concatenate([owned_x[:, :, :1, :] + incoming_x, owned_x[:, :, 1:, :]], axis=2)
    incoming_y = shifted(owned_x[..., rows_y:], "gy", 1)
    emission = owned_x[..., :rows_y]
    emission = jnp.concatenate([emission[..., :1] + incoming_y, emission[..., 1:]], axis=3)
    state = radiation
    ion = ion_fraction
    for step in range(SUBSTEPS):
        padded = padded_2(state, (("gx", 3), ("gy", 4)), 1)
        state = add_source(transport(padded), emission)
        state, ion = chemistry(state, ion, density)
    return (state, ion)


def solution(mesh):
    return jax.shard_map(
        on_device,
        mesh=mesh,
        in_specs=(
            P(None, None, None, "gx", "gy"),
            P(None, "gx", "gy"),
            P(None, "gx", "gy"),
            P("gx", "gy", None, None),
            P("gx", "gy", None, None),
            P("gx", "gy", None, None),
            P("gx", "gy"),
        ),
        out_specs=(P(None, None, None, "gx", "gy"), P(None, "gx", "gy")),
        check_vma=False,
    )
```

profile of v0, /device:TPU:0, one launch (start us, length us, event | category | flops | bytes accessed | tf_op | source)
XLA Modules:
  0.0 101.0 jit_solution(4768525669086915782)
XLA Ops:
  0.6 1.1 %fusion.166 = (f32[2,4,8,1,128]{4,3,2,0,1:T(1,128)S(1)}, f32[2,4,8,1,128]{4,3,2,0,1:T(1,128)S(1)}) fusion(f32[2,4,8,16,128]{4,3,2,1,0:T(8,128)} %param.11), kind=kLoop, calls=%fused_computation.381 | loop fusion | bytes 131072 | tf_op jit(solution)/shard_map/slice | solution.py:28
  2.3 2.0 %collective-permute-start.1 = (f32[2,4,8,1,128]{4,3,2,0,1:T(1,128)S(1)}, f32[2,4,8,1,128]{4,3,2,0,1:T(1,128)S(1)}, u32[]{:S(2)}, u32[]{:S(2)}) collective-permute-start(f32[2,4,8,1,128]{4,3,2,0,1:T(1,128)S(1)} %get-tuple-element.122), channel_id=1, source_target_pairs={{8,0},{16,8},{24,16},{0,24},{9,1},{17,9},{25,17},{1,25},{10,2},{18... | collective-permute-start | bytes 98312 | tf_op jit(solution)/shard_map/ppermute | solution.py:30
  4.3 0.7 fusion.167
  5.1 0.7 fusion.168
  6.5 0.7 bitcast_multiply_fusion.4
  7.7 0.7 collective-permute-start.4
  8.4 0.8 broadcast_subtract_fusion.11
  9.3 1.7 %collective-permute-done.4 = f32[2,8,1,129]{3,2,1,0:T(1,128)S(1)} collective-permute-done((f32[2,8,1,129]{3,2,1,0:T(1,128)S(1)}, f32[2,8,1,129]{3,2,1,0:T(1,128)S(1)}, u32[]{:S(2)}, u32[]{:S(2)}) %collective-permute-start.4) | collective-permute-done | bytes 8288 | tf_op jit(solution)/shard_map/ppermute | solution.py:18
  11.1 2.3 %collective-permute-start.5 = (f32[2,8,16,1]{3,2,1,0:T(8,128)S(1)}, f32[2,8,16,1]{3,2,1,0:T(8,128)S(1)}, u32[]{:S(2)}, u32[]{:S(2)}) collective-permute-start(f32[2,8,16,1]{3,2,1,0:T(8,128)S(1)} %fusion.68), channel_id=1, source_target_pairs={{0,1},{1,2},{2,3},{3,4},{4,5},{5,6},{6,7},{7,0},{8,9},{9,10},{10,1... | collective-permute-start | bytes 3080 | tf_op jit(solution)/shard_map/ppermute | solution.py:18
  14.3 1.6 %collective-permute-start.2 = (f32[2,4,8,18,1]{3,2,4,1,0:T(8,128)S(1)}, f32[2,4,8,18,1]{3,2,4,1,0:T(8,128)S(1)}, u32[]{:S(2)}, u32[]{:S(2)}) collective-permute-start(f32[2,4,8,18,1]{3,2,4,1,0:T(8,128)S(1)} %copy.29), channel_id=1, source_target_pairs={{0,1},{1,2},{2,3},{3,4},{4,5},{5,6},{6,7},{7,0},{8,9},{9,10},{10,1... | collective-permute-start | bytes 13832 | tf_op jit(solution)/shard_map/ppermute | solution.py:27
  16.3 3.2 %collective-permute-start.3 = (f32[2,4,8,18,1]{3,2,4,1,0:T(8,128)S(1)}, f32[2,4,8,18,1]{3,2,4,1,0:T(8,128)S(1)}, u32[]{:S(2)}, u32[]{:S(2)}) collective-permute-start(f32[2,4,8,18,1]{3,2,4,1,0:T(8,128)S(1)} %copy.30), channel_id=1, source_target_pairs={{1,0},{2,1},{3,2},{4,3},{5,4},{6,5},{7,6},{0,7},{9,8},{10,9},{11,1... | collective-permute-start | bytes 13832 | tf_op jit(solution)/shard_map/ppermute | solution.py:30
  19.9 1.0 collective-permute-done.2
  21.9 0.9 pad_maximum_fusion
  24.5 1.1 %fusion.22 = f32[2,4,8,18,130]{4,3,2,0,1:T(8,128)S(1)} fusion(f32[2,4,1,18,130]{4,3,2,0,1:T(8,128)S(1)} %slice.684, f32[2,4,7,18,130]{4,3,2,0,1:T(8,128)S(1)} %slice.683, f32[2,4,1,18,130]{4,3,2,0,1:T(8,128)S(1)} %slice.686, f32[2,4,7,18,130]{4,3,2,0,1:T(8,128)S(1)} %slice.685, f32[2,1,8,18,130]{4,3,2,0,1:T(8,128)S(1)} %get-tuple-element.73, ...), kind=kLoop, calls=%fused_computation.40 | loop fusion | flops 2096640 | bytes 2995200 | tf_op jit(solution)/shard_map/sub | solution.py:55
  25.5 1.2 %copy-done.2 = f32[2,4,8,18,130]{4,3,2,0,1:T(8,128)} copy-done((f32[2,4,8,18,130]{4,3,2,0,1:T(8,128)}, f32[2,4,8,18,130]{4,3,2,0,1:T(8,128)S(1)}, u32[]{:S(2)}) %copy-start.2) | copy-done | bytes 599064
  27.7 1.2 %fusion.16 = f32[2,4,8,18,129]{4,3,2,0,1:T(8,128)S(1)} fusion(f32[2,4,8,18,130]{4,3,2,0,1:T(8,128)S(1)} %get-tuple-element.138, f32[2,4,8,18,1]{4,3,2,0,1:T(8,128)S(1)} %copy.32, f32[2,4,8,1,128]{4,3,2,0,1:T(1,128)S(1)} %collective-permute-done.1, f32[2,4,8,1,128]{4,3,2,0,1:T(1,128)S(1)} %collective-permute-done, f32[2,4,8,18,1]{4,3,2,0,1:T(8,128)S(1)} %copy.31, ...), kind=kLoop, calls=%fused_computation.26 | loop fusion | flops 1634688 | bytes 2382336 | tf_op jit(solution)/shard_map/sub | solution.py:63
  29.2 1.1 %copy-done.3 = f32[2,4,8,18,130]{4,3,2,0,1:T(8,128)S(1)} copy-done((f32[2,4,8,18,130]{4,3,2,0,1:T(8,128)S(1)}, f32[2,4,8,18,130]{4,3,2,0,1:T(8,128)}, u32[]{:S(2)}) %copy-start.3) | copy-done | bytes 599064
  32.3 1.7 %collective-permute-start.7 = (f32[2,4,8,1,128]{4,3,2,0,1:T(1,128)S(1)}, f32[2,4,8,1,128]{4,3,2,0,1:T(1,128)S(1)}, u32[]{:S(2)}, u32[]{:S(2)}) collective-permute-start(f32[2,4,8,1,128]{4,3,2,0,1:T(1,128)S(1)} %get-tuple-element.120), channel_id=1, source_target_pairs={{8,0},{16,8},{24,16},{0,24},{9,1},{17,9},{25,17},{1,25},{10,2},{18... | collective-permute-start | bytes 98312 | tf_op jit(solution)/shard_map/ppermute | solution.py:30
  34.0 1.6 %collective-permute-done.6 = f32[2,4,8,1,128]{4,3,2,0,1:T(1,128)S(1)} collective-permute-done((f32[2,4,8,1,128]{4,3,2,0,1:T(1,128)S(1)}, f32[2,4,8,1,128]{4,3,2,0,1:T(1,128)S(1)}, u32[]{:S(2)}, u32[]{:S(2)}) %collective-permute-start.6) | collective-permute-done | bytes 32800 | tf_op jit(solution)/shard_map/ppermute | solution.py:27
  36.5 1.3 %collective-permute-start.8 = (f32[2,4,8,18,1]{3,2,4,1,0:T(8,128)S(1)}, f32[2,4,8,18,1]{3,2,4,1,0:T(8,128)S(1)}, u32[]{:S(2)}, u32[]{:S(2)}) collective-permute-start(f32[2,4,8,18,1]{3,2,4,1,0:T(8,128)S(1)} %copy.37), channel_id=1, source_target_pairs={{0,1},{1,2},{2,3},{3,4},{4,5},{5,6},{6,7},{7,0},{8,9},{9,10},{10,1... | collective-permute-start | bytes 13832 | tf_op jit(solution)/shard_map/ppermute | solution.py:27
  38.2 3.7 %collective-permute-start.9 = (f32[2,4,8,18,1]{3,2,4,1,0:T(8,128)S(1)}, f32[2,4,8,18,1]{3,2,4,1,0:T(8,128)S(1)}, u32[]{:S(2)}, u32[]{:S(2)}) collective-permute-start(f32[2,4,8,18,1]{3,2,4,1,0:T(8,128)S(1)} %copy.38), channel_id=1, source_target_pairs={{1,0},{2,1},{3,2},{4,3},{5,4},{6,5},{7,6},{0,7},{9,8},{10,9},{11,1... | collective-permute-start | bytes 13832 | tf_op jit(solution)/shard_map/ppermute | solution.py:30
  42.0 1.2 %collective-permute-done.8 = f32[2,4,8,18,1]{3,2,4,1,0:T(8,128)S(1)} collective-permute-done((f32[2,4,8,18,1]{3,2,4,1,0:T(8,128)S(1)}, f32[2,4,8,18,1]{3,2,4,1,0:T(8,128)S(1)}, u32[]{:S(2)}, u32[]{:S(2)}) %collective-permute-start.8) | collective-permute-done | bytes 4640 | tf_op jit(solution)/shard_map/ppermute | solution.py:27
  44.2 0.9 pad_maximum_fusion.4
  46.6 1.4 %fusion.26 = f32[2,4,8,18,130]{4,3,2,0,1:T(8,128)S(1)} fusion(f32[2,4,1,18,130]{4,3,2,0,1:T(8,128)S(1)} %slice.725, f32[2,4,7,18,130]{4,3,2,0,1:T(8,128)S(1)} %slice.724, f32[2,4,1,18,130]{4,3,2,0,1:T(8,128)S(1)} %slice.727, f32[2,4,7,18,130]{4,3,2,0,1:T(8,128)S(1)} %slice.726, f32[2,1,8,18,130]{4,3,2,0,1:T(8,128)S(1)} %get-tuple-element.65, ...), kind=kLoop, calls=%fused_computation.51 | loop fusion | flops 2246400 | bytes 2995200 | tf_op jit(solution)/shard_map/sub | solution.py:55
  48.1 1.2 %copy-done.4 = f32[2,4,8,18,130]{4,3,2,0,1:T(8,128)} copy-done((f32[2,4,8,18,130]{4,3,2,0,1:T(8,128)}, f32[2,4,8,18,130]{4,3,2,0,1:T(8,128)S(1)}, u32[]{:S(2)}) %copy-start.4) | copy-done | bytes 599064
  50.3 1.2 %fusion.11 = f32[2,4,8,18,129]{4,3,2,0,1:T(8,128)S(1)} fusion(f32[2,4,8,18,130]{4,3,2,0,1:T(8,128)S(1)} %pad_maximum_fusion.6, f32[2,4,8,18,1]{4,3,2,0,1:T(8,128)S(1)} %copy.40, f32[2,4,8,1,128]{4,3,2,0,1:T(1,128)S(1)} %collective-permute-done.7, f32[2,3,8,16,128]{4,3,2,0,1:T(8,128)S(1)} %slice_multiply_fusion.7, f32[2,1,8,16,128]{4,3,2,0,1:T(8,128)S(1)} %fusion.74, ...), kind=kLoop, calls=%fused_computation.18 | loop fusion | flops 1931904 | bytes 2382336 | tf_op jit(solution)/shard_map/sub | solution.py:63
  51.7 1.1 %copy-done.5 = f32[2,4,8,18,130]{4,3,2,0,1:T(8,128)S(1)} copy-done((f32[2,4,8,18,130]{4,3,2,0,1:T(8,128)S(1)}, f32[2,4,8,18,130]{4,3,2,0,1:T(8,128)}, u32[]{:S(2)}) %copy-start.5) | copy-done | bytes 599064
  54.5 0.8 collective-permute-start.10
  55.3 1.0 collective-permute-start.11
  56.3 1.6 %collective-permute-done.10 = f32[2,4,8,1,128]{4,3,2,0,1:T(1,128)S(1)} collective-permute-done((f32[2,4,8,1,128]{4,3,2,0,1:T(1,128)S(1)}, f32[2,4,8,1,128]{4,3,2,0,1:T(1,128)S(1)}, u32[]{:S(2)}, u32[]{:S(2)}) %collective-permute-start.10) | collective-permute-done | bytes 32800 | tf_op jit(solution)/shard_map/ppermute | solution.py:27
  59.6 4.9 %collective-permute-start.13 = (f32[2,4,8,18,1]{3,2,4,1,0:T(8,128)S(1)}, f32[2,4,8,18,1]{3,2,4,1,0:T(8,128)S(1)}, u32[]{:S(2)}, u32[]{:S(2)}) collective-permute-start(f32[2,4,8,18,1]{3,2,4,1,0:T(8,128)S(1)} %copy.44), channel_id=1, source_target_pairs={{1,0},{2,1},{3,2},{4,3},{5,4},{6,5},{7,6},{0,7},{9,8},{10,9},{11,1... | collective-permute-start | bytes 13832 | tf_op jit(solution)/shard_map/ppermute | solution.py:30
  64.5 1.1 %collective-permute-done.12 = f32[2,4,8,18,1]{3,2,4,1,0:T(8,128)S(1)} collective-permute-done((f32[2,4,8,18,1]{3,2,4,1,0:T(8,128)S(1)}, f32[2,4,8,18,1]{3,2,4,1,0:T(8,128)S(1)}, u32[]{:S(2)}, u32[]{:S(2)}) %collective-permute-start.12) | collective-permute-done | bytes 4640 | tf_op jit(solution)/shard_map/ppermute | solution.py:27
  66.7 0.9 pad_maximum_fusion.8
  69.1 1.4 %fusion.30 = f32[2,4,8,18,130]{4,3,2,0,1:T(8,128)S(1)} fusion(f32[2,4,1,18,130]{4,3,2,0,1:T(8,128)S(1)} %slice.759, f32[2,4,7,18,130]{4,3,2,0,1:T(8,128)S(1)} %slice.758, f32[2,4,1,18,130]{4,3,2,0,1:T(8,128)S(1)} %slice.761, f32[2,4,7,18,130]{4,3,2,0,1:T(8,128)S(1)} %slice.760, f32[2,1,8,18,130]{4,3,2,0,1:T(8,128)S(1)} %get-tuple-element.57, ...), kind=kLoop, calls=%fused_computation.62 | loop fusion | flops 2246400 | bytes 2995200 | tf_op jit(solution)/shard_map/sub | solution.py:55
  70.6 1.2 %copy-done.6 = f32[2,4,8,18,130]{4,3,2,0,1:T(8,128)} copy-done((f32[2,4,8,18,130]{4,3,2,0,1:T(8,128)}, f32[2,4,8,18,130]{4,3,2,0,1:T(8,128)S(1)}, u32[]{:S(2)}) %copy-start.6) | copy-done | bytes 599064
  72.7 1.2 %fusion.6 = f32[2,4,8,18,129]{4,3,2,0,1:T(8,128)S(1)} fusion(f32[2,4,8,18,130]{4,3,2,0,1:T(8,128)S(1)} %pad_maximum_fusion.10, f32[2,4,8,18,1]{4,3,2,0,1:T(8,128)S(1)} %copy.46, f32[2,4,8,1,128]{4,3,2,0,1:T(1,128)S(1)} %collective-permute-done.11, f32[2,3,8,16,128]{4,3,2,0,1:T(8,128)S(1)} %slice_multiply_fusion.6, f32[2,1,8,16,128]{4,3,2,0,1:T(8,128)S(1)} %fusion.77, ...), kind=kLoop, calls=%fused_computation.10 | loop fusion | flops 1931904 | bytes 2382336 | tf_op jit(solution)/shard_map/sub | solution.py:63
  74.2 1.1 %copy-done.7 = f32[2,4,8,18,130]{4,3,2,0,1:T(8,128)S(1)} copy-done((f32[2,4,8,18,130]{4,3,2,0,1:T(8,128)S(1)}, f32[2,4,8,18,130]{4,3,2,0,1:T(8,128)}, u32[]{:S(2)}) %copy-start.7) | copy-done | bytes 599064
  77.0 0.8 collective-permute-start.14
  77.8 1.0 collective-permute-start.15
  78.8 1.6 %collective-permute-done.14 = f32[2,4,8,1,128]{4,3,2,0,1:T(1,128)S(1)} collective-permute-done((f32[2,4,8,1,128]{4,3,2,0,1:T(1,128)S(1)}, f32[2,4,8,1,128]{4,3,2,0,1:T(1,128)S(1)}, u32[]{:S(2)}, u32[]{:S(2)}) %collective-permute-start.14) | collective-permute-done | bytes 32800 | tf_op jit(solution)/shard_map/ppermute | solution.py:27
  81.8 5.2 %collective-permute-start.17 = (f32[2,4,8,18,1]{3,2,4,1,0:T(8,128)S(1)}, f32[2,4,8,18,1]{3,2,4,1,0:T(8,128)S(1)}, u32[]{:S(2)}, u32[]{:S(2)}) collective-permute-start(f32[2,4,8,18,1]{3,2,4,1,0:T(8,128)S(1)} %copy.50), channel_id=1, source_target_pairs={{1,0},{2,1},{3,2},{4,3},{5,4},{6,5},{7,6},{0,7},{9,8},{10,9},{11,1... | collective-permute-start | bytes 13832 | tf_op jit(solution)/shard_map/ppermute | solution.py:30
  87.1 1.1 %collective-permute-done.16 = f32[2,4,8,18,1]{3,2,4,1,0:T(8,128)S(1)} collective-permute-done((f32[2,4,8,18,1]{3,2,4,1,0:T(8,128)S(1)}, f32[2,4,8,18,1]{3,2,4,1,0:T(8,128)S(1)}, u32[]{:S(2)}, u32[]{:S(2)}) %collective-permute-start.16) | collective-permute-done | bytes 4640 | tf_op jit(solution)/shard_map/ppermute | solution.py:27
  89.2 0.9 pad_maximum_fusion.12
  91.6 1.4 %fusion.34 = f32[2,4,8,18,130]{4,3,2,0,1:T(8,128)S(1)} fusion(f32[2,4,1,18,130]{4,3,2,0,1:T(8,128)S(1)} %slice.793, f32[2,4,7,18,130]{4,3,2,0,1:T(8,128)S(1)} %slice.792, f32[2,4,1,18,130]{4,3,2,0,1:T(8,128)S(1)} %slice.795, f32[2,4,7,18,130]{4,3,2,0,1:T(8,128)S(1)} %slice.794, f32[2,1,8,18,130]{4,3,2,0,1:T(8,128)S(1)} %get-tuple-element.49, ...), kind=kLoop, calls=%fused_computation.73 | loop fusion | flops 2246400 | bytes 2995200 | tf_op jit(solution)/shard_map/sub | solution.py:55
  93.1 1.2 %copy-done.8 = f32[2,4,8,18,130]{4,3,2,0,1:T(8,128)} copy-done((f32[2,4,8,18,130]{4,3,2,0,1:T(8,128)}, f32[2,4,8,18,130]{4,3,2,0,1:T(8,128)S(1)}, u32[]{:S(2)}) %copy-start.8) | copy-done | bytes 599064
  95.3 1.2 %fusion.1 = f32[2,4,8,18,129]{4,3,2,0,1:T(8,128)S(1)} fusion(f32[2,4,8,18,130]{4,3,2,0,1:T(8,128)S(1)} %pad_maximum_fusion.14, f32[2,4,8,18,1]{4,3,2,0,1:T(8,128)S(1)} %copy.52, f32[2,4,8,1,128]{4,3,2,0,1:T(1,128)S(1)} %collective-permute-done.15, f32[2,3,8,16,128]{4,3,2,0,1:T(8,128)S(1)} %slice_multiply_fusion.5, f32[2,1,8,16,128]{4,3,2,0,1:T(8,128)S(1)} %fusion.80, ...), kind=kLoop, calls=%fused_computation.2 | loop fusion | flops 1931904 | bytes 2382336 | tf_op jit(solution)/shard_map/sub | solution.py:63
  96.8 1.1 %copy-done.9 = f32[2,4,8,18,130]{4,3,2,0,1:T(8,128)S(1)} copy-done((f32[2,4,8,18,130]{4,3,2,0,1:T(8,128)S(1)}, f32[2,4,8,18,130]{4,3,2,0,1:T(8,128)}, u32[]{:S(2)}) %copy-start.9) | copy-done | bytes 599064
  99.5 0.8 copy.55
  (180 shorter events, 30.2 us)
Async XLA Ops:
  0.6 12.8 %copy-start.1 = (f32[2,4,8,16,128]{4,3,2,1,0:T(8,128)S(1)}, f32[2,4,8,16,128]{4,3,2,1,0:T(8,128)}, u32[]{:S(2)}) copy-start(f32[2,4,8,16,128]{4,3,2,1,0:T(8,128)} %param.11) | copy-start | bytes 1572868
  1.8 11.6 %collective-permute-start = (f32[2,4,8,1,128]{4,3,2,0,1:T(1,128)S(1)}, f32[2,4,8,1,128]{4,3,2,0,1:T(1,128)S(1)}, u32[]{:S(2)}, u32[]{:S(2)}) collective-permute-start(f32[2,4,8,1,128]{4,3,2,0,1:T(1,128)S(1)} %get-tuple-element.121), channel_id=1, source_target_pairs={{0,8},{8,16},{16,24},{24,0},{1,9},{9,17},{17,25},{25,1},{2,10},{10... | collective-permute-start | bytes 98312 | tf_op jit(solution)/shard_map/ppermute | solution.py:27
  2.3 11.1 %collective-permute-start.1 = (f32[2,4,8,1,128]{4,3,2,0,1:T(1,128)S(1)}, f32[2,4,8,1,128]{4,3,2,0,1:T(1,128)S(1)}, u32[]{:S(2)}, u32[]{:S(2)}) collective-permute-start(f32[2,4,8,1,128]{4,3,2,0,1:T(1,128)S(1)} %get-tuple-element.122), channel_id=1, source_target_pairs={{8,0},{16,8},{24,16},{0,24},{9,1},{17,9},{25,17},{1,25},{10,2},{18... | collective-permute-start | bytes 98312 | tf_op jit(solution)/shard_map/ppermute | solution.py:30
  7.7 3.2 %collective-permute-start.4 = (f32[2,8,1,129]{3,2,1,0:T(1,128)S(1)}, f32[2,8,1,129]{3,2,1,0:T(1,128)S(1)}, u32[]{:S(2)}, u32[]{:S(2)}) collective-permute-start(f32[2,8,1,129]{3,2,1,0:T(1,128)S(1)} %slice.692), channel_id=1, source_target_pairs={{0,8},{8,16},{16,24},{24,0},{1,9},{9,17},{17,25},{25,1},{2,10},{10... | collective-permute-start | bytes 24776 | tf_op jit(solution)/shard_map/ppermute | solution.py:18
  11.1 8.8 %collective-permute-start.5 = (f32[2,8,16,1]{3,2,1,0:T(8,128)S(1)}, f32[2,8,16,1]{3,2,1,0:T(8,128)S(1)}, u32[]{:S(2)}, u32[]{:S(2)}) collective-permute-start(f32[2,8,16,1]{3,2,1,0:T(8,128)S(1)} %fusion.68), channel_id=1, source_target_pairs={{0,1},{1,2},{2,3},{3,4},{4,5},{5,6},{6,7},{7,0},{8,9},{9,10},{10,1... | collective-permute-start | bytes 3080 | tf_op jit(solution)/shard_map/ppermute | solution.py:18
  14.3 6.6 %collective-permute-start.2 = (f32[2,4,8,18,1]{3,2,4,1,0:T(8,128)S(1)}, f32[2,4,8,18,1]{3,2,4,1,0:T(8,128)S(1)}, u32[]{:S(2)}, u32[]{:S(2)}) collective-permute-start(f32[2,4,8,18,1]{3,2,4,1,0:T(8,128)S(1)} %copy.29), channel_id=1, source_target_pairs={{0,1},{1,2},{2,3},{3,4},{4,5},{5,6},{6,7},{7,0},{8,9},{9,10},{10,1... | collective-permute-start | bytes 13832 | tf_op jit(solution)/shard_map/ppermute | solution.py:27
  16.3 5.1 %collective-permute-start.3 = (f32[2,4,8,18,1]{3,2,4,1,0:T(8,128)S(1)}, f32[2,4,8,18,1]{3,2,4,1,0:T(8,128)S(1)}, u32[]{:S(2)}, u32[]{:S(2)}) collective-permute-start(f32[2,4,8,18,1]{3,2,4,1,0:T(8,128)S(1)} %copy.30), channel_id=1, source_target_pairs={{1,0},{2,1},{3,2},{4,3},{5,4},{6,5},{7,6},{0,7},{9,8},{10,9},{11,1... | collective-permute-start | bytes 13832 | tf_op jit(solution)/shard_map/ppermute | solution.py:30
  25.5 1.2 %copy-start.2 = (f32[2,4,8,18,130]{4,3,2,0,1:T(8,128)}, f32[2,4,8,18,130]{4,3,2,0,1:T(8,128)S(1)}, u32[]{:S(2)}) copy-start(f32[2,4,8,18,130]{4,3,2,0,1:T(8,128)S(1)} %fusion.22) | copy-start | bytes 1797124
  28.9 1.4 %copy-start.3 = (f32[2,4,8,18,130]{4,3,2,0,1:T(8,128)S(1)}, f32[2,4,8,18,130]{4,3,2,0,1:T(8,128)}, u32[]{:S(2)}) copy-start(f32[2,4,8,18,130]{4,3,2,0,1:T(8,128)} %copy-done.2) | copy-start | bytes 1797124
  28.9 1.8 %slice-start = ((f32[2,4,8,18,130]{4,3,2,0,1:T(8,128)}), f32[2,4,7,18,130]{4,3,2,0,1:T(8,128)S(1)}, s32[]{:S(2)}) async-start(f32[2,4,8,18,130]{4,3,2,0,1:T(8,128)} %copy-done.2), calls=%async_computation | async-start | bytes 2752512 | tf_op jit(solution)/shard_map/jit(_roll_static)/slice | solution.py:56
  28.9 1.9 %slice-start.1 = ((f32[2,4,8,18,130]{4,3,2,0,1:T(8,128)}), f32[2,4,1,18,130]{4,3,2,0,1:T(8,128)S(1)}, s32[]{:S(2)}) async-start(f32[2,4,8,18,130]{4,3,2,0,1:T(8,128)} %copy-done.2), calls=%async_computation.1 | async-start | bytes 393216 | tf_op jit(solution)/shard_map/jit(_roll_static)/slice | solution.py:56
  30.7 0.8 copy-start
  30.7 0.8 copy-start.11
  30.7 0.8 copy-start.12
  30.7 1.0 copy-start.10
  32.2 3.4 %collective-permute-start.6 = (f32[2,4,8,1,128]{4,3,2,0,1:T(1,128)S(1)}, f32[2,4,8,1,128]{4,3,2,0,1:T(1,128)S(1)}, u32[]{:S(2)}, u32[]{:S(2)}) collective-permute-start(f32[2,4,8,1,128]{4,3,2,0,1:T(1,128)S(1)} %get-tuple-element.119), channel_id=1, source_target_pairs={{0,8},{8,16},{16,24},{24,0},{1,9},{9,17},{17,25},{25,1},{2,10},{10... | collective-permute-start | bytes 98312 | tf_op jit(solution)/shard_map/ppermute | solution.py:27
  32.3 3.3 %collective-permute-start.7 = (f32[2,4,8,1,128]{4,3,2,0,1:T(1,128)S(1)}, f32[2,4,8,1,128]{4,3,2,0,1:T(1,128)S(1)}, u32[]{:S(2)}, u32[]{:S(2)}) collective-permute-start(f32[2,4,8,1,128]{4,3,2,0,1:T(1,128)S(1)} %get-tuple-element.120), channel_id=1, source_target_pairs={{8,0},{16,8},{24,16},{0,24},{9,1},{17,9},{25,17},{1,25},{10,2},{18... | collective-permute-start | bytes 98312 | tf_op jit(solution)/shard_map/ppermute | solution.py:30
  36.5 6.6 %collective-permute-start.8 = (f32[2,4,8,18,1]{3,2,4,1,0:T(8,128)S(1)}, f32[2,4,8,18,1]{3,2,4,1,0:T(8,128)S(1)}, u32[]{:S(2)}, u32[]{:S(2)}) collective-permute-start(f32[2,4,8,18,1]{3,2,4,1,0:T(8,128)S(1)} %copy.37), channel_id=1, source_target_pairs={{0,1},{1,2},{2,3},{3,4},{4,5},{5,6},{6,7},{7,0},{8,9},{9,10},{10,1... | collective-permute-start | bytes 13832 | tf_op jit(solution)/shard_map/ppermute | solution.py:27
  38.2 5.4 %collective-permute-start.9 = (f32[2,4,8,18,1]{3,2,4,1,0:T(8,128)S(1)}, f32[2,4,8,18,1]{3,2,4,1,0:T(8,128)S(1)}, u32[]{:S(2)}, u32[]{:S(2)}) collective-permute-start(f32[2,4,8,18,1]{3,2,4,1,0:T(8,128)S(1)} %copy.38), channel_id=1, source_target_pairs={{1,0},{2,1},{3,2},{4,3},{5,4},{6,5},{7,6},{0,7},{9,8},{10,9},{11,1... | collective-permute-start | bytes 13832 | tf_op jit(solution)/shard_map/ppermute | solution.py:30
  48.0 1.2 %copy-start.4 = (f32[2,4,8,18,130]{4,3,2,0,1:T(8,128)}, f32[2,4,8,18,130]{4,3,2,0,1:T(8,128)S(1)}, u32[]{:S(2)}) copy-start(f32[2,4,8,18,130]{4,3,2,0,1:T(8,128)S(1)} %fusion.26) | copy-start | bytes 1797124
  51.4 1.4 %copy-start.5 = (f32[2,4,8,18,130]{4,3,2,0,1:T(8,128)S(1)}, f32[2,4,8,18,130]{4,3,2,0,1:T(8,128)}, u32[]{:S(2)}) copy-start(f32[2,4,8,18,130]{4,3,2,0,1:T(8,128)} %copy-done.4) | copy-start | bytes 1797124
  51.4 1.8 %slice-start.2 = ((f32[2,4,8,18,130]{4,3,2,0,1:T(8,128)}), f32[2,4,7,18,130]{4,3,2,0,1:T(8,128)S(1)}, s32[]{:S(2)}) async-start(f32[2,4,8,18,130]{4,3,2,0,1:T(8,128)} %copy-done.4), calls=%async_computation.2 | async-start | bytes 2752512 | tf_op jit(solution)/shard_map/jit(_roll_static)/slice | solution.py:56
  51.4 1.9 %slice-start.3 = ((f32[2,4,8,18,130]{4,3,2,0,1:T(8,128)}), f32[2,4,1,18,130]{4,3,2,0,1:T(8,128)S(1)}, s32[]{:S(2)}) async-start(f32[2,4,8,18,130]{4,3,2,0,1:T(8,128)} %copy-done.4), calls=%async_computation.3 | async-start | bytes 393216 | tf_op jit(solution)/shard_map/jit(_roll_static)/slice | solution.py:56
  54.5 3.4 %collective-permute-start.10 = (f32[2,4,8,1,128]{4,3,2,0,1:T(1,128)S(1)}, f32[2,4,8,1,128]{4,3,2,0,1:T(1,128)S(1)}, u32[]{:S(2)}, u32[]{:S(2)}) collective-permute-start(f32[2,4,8,1,128]{4,3,2,0,1:T(1,128)S(1)} %get-tuple-element.117), channel_id=1, source_target_pairs={{0,8},{8,16},{16,24},{24,0},{1,9},{9,17},{17,25},{25,1},{2,10},{10... | collective-permute-start | bytes 98312 | tf_op jit(solution)/shard_map/ppermute | solution.py:27
  55.3 2.6 %collective-permute-start.11 = (f32[2,4,8,1,128]{4,3,2,0,1:T(1,128)S(1)}, f32[2,4,8,1,128]{4,3,2,0,1:T(1,128)S(1)}, u32[]{:S(2)}, u32[]{:S(2)}) collective-permute-start(f32[2,4,8,1,128]{4,3,2,0,1:T(1,128)S(1)} %get-tuple-element.118), channel_id=1, source_target_pairs={{8,0},{16,8},{24,16},{0,24},{9,1},{17,9},{25,17},{1,25},{10,2},{18... | collective-permute-start | bytes 98312 | tf_op jit(solution)/shard_map/ppermute | solution.py:30
  58.8 6.8 %collective-permute-start.12 = (f32[2,4,8,18,1]{3,2,4,1,0:T(8,128)S(1)}, f32[2,4,8,18,1]{3,2,4,1,0:T(8,128)S(1)}, u32[]{:S(2)}, u32[]{:S(2)}) collective-permute-start(f32[2,4,8,18,1]{3,2,4,1,0:T(8,128)S(1)} %copy.43), channel_id=1, source_target_pairs={{0,1},{1,2},{2,3},{3,4},{4,5},{5,6},{6,7},{7,0},{8,9},{9,10},{10,1... | collective-permute-start | bytes 13832 | tf_op jit(solution)/shard_map/ppermute | solution.py:27
  59.6 6.6 %collective-permute-start.13 = (f32[2,4,8,18,1]{3,2,4,1,0:T(8,128)S(1)}, f32[2,4,8,18,1]{3,2,4,1,0:T(8,128)S(1)}, u32[]{:S(2)}, u32[]{:S(2)}) collective-permute-start(f32[2,4,8,18,1]{3,2,4,1,0:T(8,128)S(1)} %copy.44), channel_id=1, source_target_pairs={{1,0},{2,1},{3,2},{4,3},{5,4},{6,5},{7,6},{0,7},{9,8},{10,9},{11,1... | collective-permute-start | bytes 13832 | tf_op jit(solution)/shard_map/ppermute | solution.py:30
  70.5 1.2 %copy-start.6 = (f32[2,4,8,18,130]{4,3,2,0,1:T(8,128)}, f32[2,4,8,18,130]{4,3,2,0,1:T(8,128)S(1)}, u32[]{:S(2)}) copy-start(f32[2,4,8,18,130]{4,3,2,0,1:T(8,128)S(1)} %fusion.30) | copy-start | bytes 1797124
  73.9 1.4 %copy-start.7 = (f32[2,4,8,18,130]{4,3,2,0,1:T(8,128)S(1)}, f32[2,4,8,18,130]{4,3,2,0,1:T(8,128)}, u32[]{:S(2)}) copy-start(f32[2,4,8,18,130]{4,3,2,0,1:T(8,128)} %copy-done.6) | copy-start | bytes 1797124
  73.9 1.8 %slice-start.4 = ((f32[2,4,8,18,130]{4,3,2,0,1:T(8,128)}), f32[2,4,7,18,130]{4,3,2,0,1:T(8,128)S(1)}, s32[]{:S(2)}) async-start(f32[2,4,8,18,130]{4,3,2,0,1:T(8,128)} %copy-done.6), calls=%async_computation.4 | async-start | bytes 2752512 | tf_op jit(solution)/shard_map/jit(_roll_static)/slice | solution.py:56
  73.9 1.9 %slice-start.5 = ((f32[2,4,8,18,130]{4,3,2,0,1:T(8,128)}), f32[2,4,1,18,130]{4,3,2,0,1:T(8,128)S(1)}, s32[]{:S(2)}) async-start(f32[2,4,8,18,130]{4,3,2,0,1:T(8,128)} %copy-done.6), calls=%async_computation.5 | async-start | bytes 393216 | tf_op jit(solution)/shard_map/jit(_roll_static)/slice | solution.py:56
  77.0 3.4 %collective-permute-start.14 = (f32[2,4,8,1,128]{4,3,2,0,1:T(1,128)S(1)}, f32[2,4,8,1,128]{4,3,2,0,1:T(1,128)S(1)}, u32[]{:S(2)}, u32[]{:S(2)}) collective-permute-start(f32[2,4,8,1,128]{4,3,2,0,1:T(1,128)S(1)} %get-tuple-element.115), channel_id=1, source_target_pairs={{0,8},{8,16},{16,24},{24,0},{1,9},{9,17},{17,25},{25,1},{2,10},{10... | collective-permute-start | bytes 98312 | tf_op jit(solution)/shard_map/ppermute | solution.py:27
  77.8 2.6 %collective-permute-start.15 = (f32[2,4,8,1,128]{4,3,2,0,1:T(1,128)S(1)}, f32[2,4,8,1,128]{4,3,2,0,1:T(1,128)S(1)}, u32[]{:S(2)}, u32[]{:S(2)}) collective-permute-start(f32[2,4,8,1,128]{4,3,2,0,1:T(1,128)S(1)} %get-tuple-element.116), channel_id=1, source_target_pairs={{8,0},{16,8},{24,16},{0,24},{9,1},{17,9},{25,17},{1,25},{10,2},{18... | collective-permute-start | bytes 98312 | tf_op jit(solution)/shard_map/ppermute | solution.py:30
  81.3 6.9 %collective-permute-start.16 = (f32[2,4,8,18,1]{3,2,4,1,0:T(8,128)S(1)}, f32[2,4,8,18,1]{3,2,4,1,0:T(8,128)S(1)}, u32[]{:S(2)}, u32[]{:S(2)}) collective-permute-start(f32[2,4,8,18,1]{3,2,4,1,0:T(8,128)S(1)} %copy.49), channel_id=1, source_target_pairs={{0,1},{1,2},{2,3},{3,4},{4,5},{5,6},{6,7},{7,0},{8,9},{9,10},{10,1... | collective-permute-start | bytes 13832 | tf_op jit(solution)/shard_map/ppermute | solution.py:27
  81.8 6.9 %collective-permute-start.17 = (f32[2,4,8,18,1]{3,2,4,1,0:T(8,128)S(1)}, f32[2,4,8,18,1]{3,2,4,1,0:T(8,128)S(1)}, u32[]{:S(2)}, u32[]{:S(2)}) collective-permute-start(f32[2,4,8,18,1]{3,2,4,1,0:T(8,128)S(1)} %copy.50), channel_id=1, source_target_pairs={{1,0},{2,1},{3,2},{4,3},{5,4},{6,5},{7,6},{0,7},{9,8},{10,9},{11,1... | collective-permute-start | bytes 13832 | tf_op jit(solution)/shard_map/ppermute | solution.py:30
  93.1 1.2 %copy-start.8 = (f32[2,4,8,18,130]{4,3,2,0,1:T(8,128)}, f32[2,4,8,18,130]{4,3,2,0,1:T(8,128)S(1)}, u32[]{:S(2)}) copy-start(f32[2,4,8,18,130]{4,3,2,0,1:T(8,128)S(1)} %fusion.34) | copy-start | bytes 1797124
  96.4 1.4 %copy-start.9 = (f32[2,4,8,18,130]{4,3,2,0,1:T(8,128)S(1)}, f32[2,4,8,18,130]{4,3,2,0,1:T(8,128)}, u32[]{:S(2)}) copy-start(f32[2,4,8,18,130]{4,3,2,0,1:T(8,128)} %copy-done.8) | copy-start | bytes 1797124
  96.5 1.8 %slice-start.6 = ((f32[2,4,8,18,130]{4,3,2,0,1:T(8,128)}), f32[2,4,7,18,130]{4,3,2,0,1:T(8,128)S(1)}, s32[]{:S(2)}) async-start(f32[2,4,8,18,130]{4,3,2,0,1:T(8,128)} %copy-done.8), calls=%async_computation.6 | async-start | bytes 2752512 | tf_op jit(solution)/shard_map/jit(_roll_static)/slice | solution.py:56
  96.5 1.9 %slice-start.7 = ((f32[2,4,8,18,130]{4,3,2,0,1:T(8,128)}), f32[2,4,1,18,130]{4,3,2,0,1:T(8,128)S(1)}, s32[]{:S(2)}) async-start(f32[2,4,8,18,130]{4,3,2,0,1:T(8,128)} %copy-done.8), calls=%async_computation.7 | async-start | bytes 393216 | tf_op jit(solution)/shard_map/jit(_roll_static)/slice | solution.py:56
where the time goes:
time: 102 us; the launch traced here: 101 us
  starting transfers between devices  31.1 us (30%)
  other arithmetic  29.4 us (29%)
  local copies, waits for them, and re-layouts  26.7 us (26%)
  waiting for transfers between devices  11.2 us (11%)
  between operations  2.15 us (2%)
    ppermute x8, starting transfers between devices, padded_2(): lax.ppermute(lax.slice_in_dim(block, 0, width, axis=dim), axis, backward)  22.8 us
    unnamed x27, local copies, waits for them, and re-layouts  10.1 us
    ppermute x8, waiting for transfers between devices, padded_2(): lax.ppermute(lax.slice_in_dim(block, block.shape[dim] - width, None, axis...  9.13 us
    ppermute x8, starting transfers between devices, padded_2(): lax.ppermute(lax.slice_in_dim(block, block.shape[dim] - width, None, axis...  5.39 us
    sub x4, other arithmetic, transport(): 0.5 * (phys_z + jnp.roll(phys_z, -1, 2))  5.32 us
    sub x4, other arithmetic, transport(): 0.5 * (phys_y[..., :-1] + phys_y[..., 1:])  4.62 us
    concatenate x8, other arithmetic, padded_2(): block = jnp.concatenate([low, block, high], axis=dim)  4.27 us
    slice x9, local copies, waits for them, and re-layouts, padded_2(): lax.slice_in_dim(block, block.shape[dim] - width, None, axis=dim)  4.18 us
  transfers between devices with their start and end apart: 18, of which 9 were waited for; matrix products, arithmetic and copies ran while one was open for 9% of the time, Pallas kernels for 0%

commit v1 on v0

v1 whole, which is shorter than its diff:
```python
import jax
import jax.numpy as jnp
from jax import lax
from jax.experimental import pallas as pl
from jax.experimental.pallas import tpu as pltpu
from jax.sharding import PartitionSpec as P

SUBSTEPS = 4
CHEM_ITERS = 3
DT = 0.3
ALPHA = 0.4
SIGMA = (1.5, 0.5)

HALO = SUBSTEPS
INNER = HALO - 1


def neighbour_pairs(count, parity):
    return [(i, (i + 1) % count if i % 2 == parity else (i - 1) % count) for i in range(count)]


def halo_rows(fields_full, fields_inner, depth):
    full = fields_full * HALO * depth
    return full, full + fields_inner * INNER * depth


def star_table(lum_ref, cell_ref, off_ref, count_ref):
    slots = lum_ref.shape[3]
    slot = lax.broadcasted_iota(jnp.int32, (1, slots), 1)
    live = (slot < count_ref[0, 0]).astype(jnp.float32)
    lum = [lum_ref[0, 0, g : g + 1, :] * live for g in range(lum_ref.shape[2])]
    cell = [cell_ref[0, 0, a : a + 1, :].astype(jnp.float32) for a in range(3)]
    off = [off_ref[0, 0, a : a + 1, :] for a in range(3)]
    return lum, cell, off


def deposit(stars, rows, depth, width):
    lum, cell, off = stars
    slots = lum[0].shape[1]
    z = lax.broadcasted_iota(jnp.int32, (depth, slots), 0).astype(jnp.float32)
    upper = cell[2] + 1.0
    upper = jnp.where(upper == float(depth), 0.0, upper)
    weight_z = jnp.where(z == cell[2], 1.0 - off[2], 0.0) + jnp.where(z == upper, off[2], 0.0)
    y = lax.broadcasted_iota(jnp.int32, (2 * width, slots), 0).astype(jnp.float32)
    weight_y = jnp.where(y == cell[1], 1.0 - off[1], 0.0) + jnp.where(y == cell[1] + 1.0, off[1], 0.0)
    left = []
    for light in lum:
        for x in rows:
            weight_x = jnp.where(cell[0] == float(x), 1.0 - off[0], 0.0)
            weight_x = weight_x + jnp.where(cell[0] == float(x - 1), off[0], 0.0)
            left.append(weight_z * (weight_x * light))
    return lax.dot_general(
        jnp.concatenate(left, axis=0),
        weight_y,
        (((1,), (1,)), ((), ())),
        precision=lax.Precision.HIGHEST,
        preferred_element_type=jnp.float32,
    )


def strip_lane():
    return lax.broadcasted_iota(jnp.int32, (8, 128), 1)


def to_strip(plane, group, lane, base):
    low = pltpu.roll(plane, (16 * group + 4) % 128, 1)
    high = pltpu.roll(plane, (16 * group + 12) % 128, 1)
    base = jnp.where((lane >= 16 * group) & (lane < 16 * group + 8), low, base)
    return jnp.where((lane >= 16 * group + 8) & (lane < 16 * group + 16), high, base)


def pack_kernel(rad, ion, den, lum_ref, cell_ref, off_ref, count_ref, out0, out1):
    even = lax.rem(lax.axis_index("gx"), 2) == 0
    groups, comps, depth, rows_x, width = rad.shape
    at = 0

    def put(high, low):
        nonlocal at
        out0[pl.ds(at, depth), :] = jnp.where(even, high, low)
        out1[pl.ds(at, depth), :] = jnp.where(even, low, high)
        at += depth

    for g in range(groups):
        for c in range(comps):
            for i in range(HALO):
                put(rad[g, c, :, rows_x - HALO + i, :], rad[g, c, :, i, :])
    for ref in (ion, den):
        for i in range(INNER):
            put(ref[:, rows_x - INNER + i, :], ref[:, i, :])
    lum, cell, off = star_table(lum_ref, cell_ref, off_ref, count_ref)
    table = jnp.concatenate(lum + cell + off, axis=0)
    for part in range(table.shape[1] // width):
        piece = table[:, part * width : (part + 1) * width]
        put(piece, piece)


def own_kernel(rad, ion, den, lum_ref, cell_ref, off_ref, count_ref, emis, strips):
    groups, comps, depth, rows_x, width = rad.shape
    stars = star_table(lum_ref, cell_ref, off_ref, count_ref)
    emis[...] = deposit(stars, range(rows_x + 1), depth, width)
    lane = strip_lane()
    fields = [(lambda x, g=g, c=c: rad[g, c, :, x, :]) for g in range(groups) for c in range(comps)]
    fields += [lambda x: ion[:, x, :], lambda x: den[:, x, :]]
    for f, read in enumerate(fields):
        for v in range(rows_x // 8):
            acc = jnp.zeros((8, 128), jnp.float32)
            for group in range(8):
                acc = to_strip(read(8 * v + group), group, lane, acc)
            strips[f, v] = acc


def edge_kernel(from0, from1, emis, strips_own, sent, own_e, centre_e):
    even = lax.rem(lax.axis_index("gx"), 2) == 0
    fields, owned, depth, width = strips_own.shape
    groups = own_e.shape[0]
    rows_x = 8 * owned
    lane = strip_lane()
    full, inner = halo_rows(fields - 2, 2, depth)

    def beside(at, size=None):
        size = depth if size is None else size
        first, second = from0[pl.ds(at, size), :], from1[pl.ds(at, size), :]
        return jnp.where(even, second, first), jnp.where(even, first, second)

    for f in range(fields):
        acc = jnp.zeros((8, 128), jnp.float32)
        for i in range(HALO):
            if f < fields - 2:
                below, above = beside((f * HALO + i) * depth)
                low_at, high_at = i, i + HALO
            elif i < INNER:
                below, above = beside(full + ((f - fields + 2) * INNER + i) * depth)
                low_at, high_at = i, i + HALO + 1
            else:
                continue
            acc = to_strip(above, low_at, lane, acc)
            acc = to_strip(below, high_at, lane, acc)
        for v in range(owned):
            sent[f, v] = strips_own[f, v]
        sent[f, owned] = acc

    parts = [beside(inner + p * depth) for p in range((from0.shape[0] - inner) // depth)]

    def stars_of(side):
        table = jnp.concatenate([part[side] for part in parts], axis=1)
        row = [table[k : k + 1, :] for k in range(table.shape[0])]
        return row[:groups], row[groups : groups + 3], row[groups + 3 : groups + 6]

    low_rows = list(range(rows_x - INNER, rows_x + 1))
    high_rows = list(range(INNER))
    below_e = deposit(stars_of(0), low_rows, depth, width)
    above_e = deposit(stars_of(1), high_rows, depth, width)

    def row_of(table, count, g, index, half):
        start = (g * count + index) * depth
        return table[start : start + depth, half * width : (half + 1) * width]

    def emission(g, x, half):
        parts = []
        if 0 <= x <= rows_x:
            start = (g * (rows_x + 1) + x) * depth
            parts.append(emis[start : start + depth, half * width : (half + 1) * width])
        if x <= 0:
            parts.append(row_of(below_e, len(low_rows), g, x + INNER, half))
        if x >= rows_x:
            parts.append(row_of(above_e, len(high_rows), g, x - rows_x, half))
        return sum(parts[1:], parts[0])

    for g in range(groups):
        acc_sent = [jnp.zeros((8, 128), jnp.float32)] * (owned + 1)
        acc_own = [jnp.zeros((8, 128), jnp.float32)] * (owned + 1)
        for x in range(-INNER, rows_x + INNER):
            row = x % (rows_x + 8)
            v, group = row // 8, row % 8
            plane, past = emission(g, x, 0), emission(g, x, 1)
            centre_e[g, x + HALO] = plane
            low = pltpu.roll(plane, (16 * group + 4) % 128, 1)
            high = pltpu.roll(plane, (16 * group + 12) % 128, 1)
            past_low = pltpu.roll(past, (16 * group + 4) % 128, 1)
            past_high = pltpu.roll(past, (16 * group + 12) % 128, 1)
            column = lane - 16 * group
            s = jnp.where((column >= 4) & (column < 8), low, acc_sent[v])
            s = jnp.where((column >= 8) & (column < 12), high, s)
            acc_sent[v] = jnp.where(column == 12, past_high, s)
            o = jnp.where((column >= 0) & (column < 4), low, acc_own[v])
            o = jnp.where((column >= 12) & (column < 16), high, o)
            acc_own[v] = jnp.where(column == 4, past_low, o)
        for v in range(owned + 1):
            sent[fields + g, v] = acc_sent[v]
            own_e[g, v] = acc_own[v]


def closure(state):
    photons, flux = state[0], state[1:]
    inverse = 1.0 / photons
    unit = [f * inverse for f in flux]
    fsq = jnp.minimum(unit[0] * unit[0] + unit[1] * unit[1] + unit[2] * unit[2], 1.0)
    square = 4.0 - 3.0 * fsq
    root = square * lax.rsqrt(square)
    shape_term = 3.0 / (2.0 + root)
    diag = (root - 1.0) * (photons * (1.0 / 3.0))
    scaled = [f * shape_term for f in flux]
    xx, yy, zz = (scaled[a] * unit[a] + diag for a in range(3))
    xy, xz, yz = scaled[0] * unit[1], scaled[0] * unit[2], scaled[1] * unit[2]
    return ((flux[0], xx, xy, xz), (flux[1], xy, yy, yz), (flux[2], xz, yz, zz))


def chemistry(state, ion, dens):
    groups = len(state)
    reach = DT * dens
    loss = ALPHA * reach
    push = [state[g][0] * (DT * SIGMA[g]) for g in range(groups)]
    frac = ion
    for step in range(CHEM_ITERS):
        free = reach * (1.0 - frac)
        atten = [1.0 / (1.0 + SIGMA[g] * free) for g in range(groups)]
        gamma = sum((push[g] * atten[g] for g in range(1, groups)), push[0] * atten[0])
        frac = (ion + gamma) / (1.0 + (gamma + loss * frac))
    return [[u * atten[g] for u in state[g]] for g in range(groups)], frac


def step_kernel(
    rad, ion, den, from0, from1, sent_own, own_e, from_low, from_high, centre_e,
    rad_out, ion_out, u_ref, ion_ref, den_ref, s_ref, e_ref, t_ref,
):
    even = lax.rem(lax.axis_index("gx"), 2) == 0
    groups, comps, depth, rows_x, width = rad.shape
    tiles = sent_own.shape[1]
    cycle = 8 * tiles
    fields = groups * comps
    full, _ = halo_rows(fields, 2, depth)
    lane = strip_lane()
    column = lax.rem(lane, 16)

    def beside(at):
        first, second = from0[pl.ds(at, depth), :], from1[pl.ds(at, depth), :]
        return jnp.where(even, second, first), jnp.where(even, first, second)

    for g in range(groups):
        for c in range(comps):
            f = g * comps + c
            for x in range(rows_x):
                u_ref[f, x + HALO] = rad[g, c, :, x, :]
            for i in range(HALO):
                below, above = beside((f * HALO + i) * depth)
                u_ref[f, i] = below
                u_ref[f, rows_x + HALO + i] = above
    for k, (src, dst) in enumerate(((ion, ion_ref), (den, den_ref))):
        for x in range(rows_x):
            dst[x + HALO] = src[:, x, :]
        for i in range(INNER):
            below, above = beside(full + (k * INNER + i) * depth)
            dst[i + 1] = below
            dst[rows_x + HALO + i] = above

    from_right = (column >= 4) & (column < 8)
    from_left = (column >= 8) & (column < 12)
    for f in range(fields + 2):
        for v in range(tiles):
            s_ref[f, v] = jnp.where(
                from_right, from_high[f, v], jnp.where(from_left, from_low[f, v], sent_own[f, v])
            )
    for g in range(groups):
        for v in range(tiles):
            f = fields + 2 + g
            e = own_e[g, v] + jnp.where(from_right, from_high[f, v], 0.0)
            e = e + jnp.where((column >= 8) & (column < 13), from_low[f, v], 0.0)
            s_ref[f, v] = e * DT
        for x in range(-INNER, rows_x + INNER):
            row = x % cycle
            v, group = row // 8, row % 8
            edge = pltpu.roll(s_ref[fields + 2 + g, v], (116 - 16 * group) % 128, 1)
            e_ref[g, x + HALO] = jnp.where(lane == 0, edge, centre_e[g, x + HALO] * DT)

    keep, share = 1.0 - 3.0 * DT, 0.5 * DT
    for step in range(SUBSTEPS):
        states = [
            [[s_ref[g * comps + c, v] for c in range(comps)] for g in range(groups)]
            for v in range(tiles)
        ]
        phys = [[closure(states[v][g]) for g in range(groups)] for v in range(tiles)]
        for v in range(tiles):
            for g in range(groups):
                for c in range(comps):
                    u, f = states[v][g][c], phys[v][g][1][c]
                    t_ref[g * comps + c, v] = jnp.where(
                        column == 11, u + f, pltpu.roll(u - f, 6, 1)
                    )
        if step < SUBSTEPS - 1:
            for v in range(tiles):
                new = []
                for g in range(groups):
                    comp = []
                    for c in range(comps):
                        u = states[v][g][c]
                        fx, fy, fz = (phys[v][g][a][c] for a in range(3))
                        vn, vp = (v + 1) % tiles, (v - 1) % tiles
                        down, here_d = states[vn][g][c] - phys[vn][g][0][c], u - fx
                        up, here_u = states[vp][g][c] + phys[vp][g][0][c], u + fx
                        total = jnp.where(
                            lane < 112, pltpu.roll(here_d, 112, 1), pltpu.roll(down, 112, 1)
                        )
                        total = total + jnp.where(
                            lane < 16, pltpu.roll(up, 16, 1), pltpu.roll(here_u, 16, 1)
                        )
                        total = total + pltpu.roll(u - fy, 127, 1) + pltpu.roll(u + fy, 1, 1)
                        total = total + pltpu.roll(u - fz, depth - 1, 0) + pltpu.roll(u + fz, 1, 0)
                        comp.append(keep * u + share * total)
                    comp[0] = comp[0] + s_ref[fields + 2 + g, v]
                    new.append(comp)
                new, frac = chemistry(new, s_ref[fields, v], s_ref[fields + 1, v])
                for g in range(groups):
                    for c in range(comps):
                        s_ref[g * comps + c, v] = new[g][c]
                s_ref[fields, v] = frac

        reach = SUBSTEPS - 1 - step

        def row_terms(x):
            row = x % cycle
            v, group = row // 8, row % 8
            up, down, rest = [], [], []
            for g in range(groups):
                state = [u_ref[g * comps + c, x + HALO] for c in range(comps)]
                px, py, pz = closure(state)
                for c in range(comps):
                    u = state[c]
                    up.append(u + px[c])
                    down.append(u - px[c])
                    if -reach <= x < rows_x + reach:
                        edge = pltpu.roll(t_ref[g * comps + c, v], (117 - 16 * group) % 128, 1)
                        total = jnp.where(lane == width - 1, edge, pltpu.roll(u - py[c], width - 1, 1))
                        total = total + jnp.where(lane == 0, edge, pltpu.roll(u + py[c], 1, 1))
                        total = total + pltpu.roll(u - pz[c], depth - 1, 0)
                        total = total + pltpu.roll(u + pz[c], 1, 0)
                        rest.append(keep * u + share * total)
            return up, down, rest

        before, _, _ = row_terms(-reach - 1)
        here, _, rest = row_terms(-reach)
        for x in range(-reach, rows_x + reach):
            after, down, rest_after = row_terms(x + 1)
            new = []
            for g in range(groups):
                comp = []
                for c in range(comps):
                    k = g * comps + c
                    comp.append(rest[k] + share * (before[k] + down[k]))
                comp[0] = comp[0] + e_ref[g, x + HALO]
                new.append(comp)
            new, frac = chemistry(new, ion_ref[x + HALO], den_ref[x + HALO])
            last = step == SUBSTEPS - 1
            for g in range(groups):
                for c in range(comps):
                    if last:
                        rad_out[g, c, :, x, :] = new[g][c]
                    else:
                        u_ref[g * comps + c, x + HALO] = new[g][c]
            if last:
                ion_out[:, x, :] = frac
            else:
                ion_ref[x + HALO] = frac
            before, here, rest = here, after, rest_after


def on_device(radiation, ion_fraction, density, star_lum, star_cell, star_offset, star_count):
    groups, comps, depth, rows_x, width = radiation.shape
    slots = star_lum.shape[3]
    if depth != 8 or width != 128 or rows_x % 8 or comps != 4 or slots % width:
        raise ValueError("tile shape")
    nx, ny = lax.axis_size("gx"), lax.axis_size("gy")
    if nx % 2:
        raise ValueError("odd axis")
    fields = groups * comps
    owned = rows_x // 8
    tiles = owned + 1
    _, inner = halo_rows(fields, 2, depth)
    halo = inner + (groups + 6) * (slots // width)
    f32 = jnp.float32
    vmem = pl.BlockSpec(memory_space=pltpu.VMEM)
    smem = pl.BlockSpec(memory_space=pltpu.SMEM)
    arrays = (radiation, ion_fraction, density, star_lum, star_cell, star_offset, star_count)
    arg_specs = [vmem] * 6 + [smem]

    to0, to1 = pl.pallas_call(
        pack_kernel,
        out_shape=[jax.ShapeDtypeStruct((halo, width), f32)] * 2,
        in_specs=arg_specs,
        name="pack_x",
    )(*arrays)
    from0 = lax.ppermute(to0, "gx", neighbour_pairs(nx, 0))
    from1 = lax.ppermute(to1, "gx", neighbour_pairs(nx, 1))
    emis, strips = pl.pallas_call(
        own_kernel,
        out_shape=[
            jax.ShapeDtypeStruct((groups * (rows_x + 1) * depth, 2 * width), f32),
            jax.ShapeDtypeStruct((fields + 2, owned, 8, width), f32),
        ],
        in_specs=arg_specs,
        cost_estimate=pl.CostEstimate(flops=30_000_000, bytes_accessed=1_000_000, transcendentals=0),
        name="own_edges",
    )(*arrays)
    sent, own_e, centre_e = pl.pallas_call(
        edge_kernel,
        out_shape=[
            jax.ShapeDtypeStruct((fields + 2 + groups, tiles, 8, width), f32),
            jax.ShapeDtypeStruct((groups, tiles, 8, width), f32),
            jax.ShapeDtypeStruct((groups, rows_x + 2 * HALO, depth, width), f32),
        ],
        in_specs=[vmem] * 4,
        name="edges",
    )(from0, from1, emis, strips)
    from_low = lax.ppermute(sent, "gy", [(i, (i + 1) % ny) for i in range(ny)])
    from_high = lax.ppermute(sent, "gy", [((i + 1) % ny, i) for i in range(ny)])
    plane = (depth, width)
    rows = rows_x + 2 * HALO
    return tuple(
        pl.pallas_call(
            step_kernel,
            out_shape=[
                jax.ShapeDtypeStruct(radiation.shape, f32),
                jax.ShapeDtypeStruct(ion_fraction.shape, f32),
            ],
            in_specs=[vmem] * 10,
            scratch_shapes=[
                pltpu.VMEM((fields, rows) + plane, f32),
                pltpu.VMEM((rows,) + plane, f32),
                pltpu.VMEM((rows,) + plane, f32),
                pltpu.VMEM((fields + 2 + groups, tiles) + plane, f32),
                pltpu.VMEM((groups, rows) + plane, f32),
                pltpu.VMEM((fields, tiles) + plane, f32),
            ],
            name="substeps",
        )(
            radiation, ion_fraction, density, from0, from1, sent, own_e, from_low, from_high, centre_e
        )
    )


def solution(mesh):
    return jax.shard_map(
        on_device,
        mesh=mesh,
        in_specs=(
            P(None, None, None, "gx", "gy"),
            P(None, "gx", "gy"),
            P(None, "gx", "gy"),
            P("gx", "gy", None, None),
            P("gx", "gy", None, None),
            P("gx", "gy", None, None),
            P("gx", "gy"),
        ),
        out_specs=(P(None, None, None, "gx", "gy"), P(None, "gx", "gy")),
        check_vma=False,
    )
```

time: 102 us -> 36.9 us (0.36)
  other arithmetic: 29.4 us -> 0 us
  starting transfers between devices: 31.1 us -> 7.25 us
  local copies, waits for them, and re-layouts: 26.7 us -> 3.2 us
  Pallas kernels: 0 us -> 13.8 us
    ppermute x18 -> x4, starting transfers between devices: 31.1 us -> 7.25 us  [the longest x1 4.14 us: on_device(): from_high = lax.ppermute(sent, 'gy', [((i + 1) % ny, i) for i in range(ny)])]
    sub x31 -> x0, other arithmetic: 15.8 us -> none  [the longest x4 5.32 us: transport(): 0.5 * (phys_z + jnp.roll(phys_z, -1, 2))]
    pallas_call x0 -> x4, Pallas kernels: none -> 13.8 us  [the longest x1 6.48 us: on_device(): pl.pallas_call(step_kernel, out_shape=[jax.ShapeDtypeStruct(radiation.sha...]
    slice x57 -> x0, local copies, waits for them, and re-layouts: 12.5 us -> none  [the longest x9 4.18 us: padded_2(): lax.slice_in_dim(block, block.shape[dim] - width, None, axis=dim)]
    unnamed x27 -> x12, local copies, waits for them, and re-layouts: 10.1 us -> 3.2 us
    concatenate x15 -> x0, other arithmetic: 4.62 us -> none  [the longest x8 4.27 us: padded_2(): block = jnp.concatenate([low, block, high], axis=dim)]
    ppermute x8 -> x0, local copies, waits for them, and re-layouts: 4.07 us -> none  [the longest x4 2.03 us: padded_2(): lax.ppermute(lax.slice_in_dim(block, block.shape[dim] - width, None, axis...]
    mul x14 -> x0, other arithmetic: 3.16 us -> none  [the longest x4 1.92 us: directional(): value = scaled * flux[:, axis_dir] * flux[:, other]]
  transfers between devices with their start and end apart: 18 -> 4, of which waited for: 9 -> 3; matrix products, arithmetic and copies ran while one was open for 9% -> 0% of each run, Pallas kernels for 0% -> 7%
where the time goes in v1:
time: 36.9 us; the launch traced here: 36.7 us
  Pallas kernels  13.8 us (37%)
  waiting for transfers between devices  11.1 us (30%)
  starting transfers between devices  7.25 us (20%)
  local copies, waits for them, and re-layouts  3.2 us (9%)
  between operations  1.3 us (4%)
    pallas_call x1, Pallas kernels, on_device(): pl.pallas_call(step_kernel, out_shape=[jax.ShapeDtypeStruct(radiation.sha...  6.48 us
    ppermute x1, waiting for transfers between devices, on_device(): from_low = lax.ppermute(sent, 'gy', [(i, (i + 1) % ny) for i in range(ny)])  4.79 us
    ppermute x1, starting transfers between devices, on_device(): from_high = lax.ppermute(sent, 'gy', [((i + 1) % ny, i) for i in range(ny)])  4.14 us
    ppermute x1, waiting for transfers between devices, on_device(): from_high = lax.ppermute(sent, 'gy', [((i + 1) % ny, i) for i in range(ny)])  4.1 us
    unnamed x12, local copies, waits for them, and re-layouts  3.2 us
    pallas_call x1, Pallas kernels, on_device(): pl.pallas_call(edge_kernel, out_shape=[jax.ShapeDtypeStruct((fields + 2 +...  2.69 us
    ppermute x1, starting transfers between devices, on_device(): from1 = lax.ppermute(to1, 'gx', neighbour_pairs(nx, 1))  2.62 us
    pallas_call x1, Pallas kernels, on_device(): pl.pallas_call(own_kernel, out_shape=[jax.ShapeDtypeStruct((groups * (row...  2.52 us
  transfers between devices with their start and end apart: 4, of which 3 were waited for; matrix products, arithmetic and copies ran while one was open for 0% of the time, Pallas kernels for 7%

profile of v1, /device:TPU:0, one launch (start us, length us, event | category | flops | bytes accessed | tf_op | source)
XLA Modules:
  0.0 36.7 jit_solution(6580513494423274558)
XLA Ops:
  1.3 0.0 copy-start.4
  1.3 1.3 %copy.9.cell_ref = s32[1,1,3,256]{3,2,1,0:T(4,128)} copy(s32[1,1,3,256]{3,1,2,0:T(1,128)} %param.11) | data formatting | bytes 6144 | tf_op args[4]
  2.6 0.0 copy-done.4
  2.6 0.6 %copy.10.off_ref = f32[1,1,3,256]{3,2,1,0:T(4,128)} copy(f32[1,1,3,256]{3,1,2,0:T(1,128)S(1)} %copy-done.4) | data formatting | bytes 6144 | tf_op args[5]
  3.2 2.1 %pack_x.1 = (f32[320,128]{1,0:T(8,128)}, f32[320,128]{1,0:T(8,128)}) custom-call(f32[2,4,8,16,128]{4,3,2,1,0:T(8,128)} %rad.5, f32[8,16,128]{2,1,0:T(8,128)} %ion.5, f32[8,16,128]{2,1,0:T(8,128)} %den.5, f32[1,1,2,256]{3,2,1,0:T(2,128)} %lum_ref.3, s32[1,1,3,256]{3,2,1,0:T(4,128)} %copy.9.cell_ref, f32[1,1,3,256]{3,2,1,0:T(4,128)} %copy.10.off_ref, ...), custom_call_target="tpu_custom_call" | custom-call | tf_op jit(solution)/shard_map/pack_x/pallas_call | solution.py:385
  5.2 0.5 %collective-permute-start = (f32[320,128]{1,0:T(8,128)}, f32[320,128]{1,0:T(8,128)S(1)}, u32[]{:S(2)}, u32[]{:S(2)}) collective-permute-start(f32[320,128]{1,0:T(8,128)} %get-tuple-element.9), channel_id=1, source_target_pairs={{0,8},{8,0},{16,24},{24,16},{1,9},{9,1},{17,25},{25,17},{2,10},{10... | collective-permute-start | bytes 491528 | tf_op jit(solution)/shard_map/ppermute | solution.py:391
  5.7 2.6 %collective-permute-start.1 = (f32[320,128]{1,0:T(8,128)}, f32[320,128]{1,0:T(8,128)S(1)}, u32[]{:S(2)}, u32[]{:S(2)}) collective-permute-start(f32[320,128]{1,0:T(8,128)} %get-tuple-element.10), channel_id=1, source_target_pairs={{0,24},{8,16},{16,8},{24,0},{1,25},{9,17},{17,9},{25,1},{2,26},{10... | collective-permute-start | bytes 491528 | tf_op jit(solution)/shard_map/ppermute | solution.py:392
  8.4 2.5 %own_edges.1 = (f32[272,256]{1,0:T(8,128)}, f32[10,2,8,128]{3,2,1,0:T(8,128)}) custom-call(f32[2,4,8,16,128]{4,3,2,1,0:T(8,128)} %rad.5, f32[8,16,128]{2,1,0:T(8,128)} %ion.5, f32[8,16,128]{2,1,0:T(8,128)} %den.5, f32[1,1,2,256]{3,2,1,0:T(2,128)} %lum_ref.3, s32[1,1,3,256]{3,2,1,0:T(4,128)} %copy.9.cell_ref, f32[1,1,3,256]{3,2,1,0:T(4,128)} %copy.10.off_ref, ...), custom_call_target="tpu_custom_call" | custom-call | flops 30000000 | bytes 1000000 | tf_op jit(solution)/shard_map/own_edges/pallas_call | solution.py:393
  10.9 0.0 collective-permute-done.from0
  10.9 0.0 copy-start
  10.9 2.3 %collective-permute-done.1.from1 = f32[320,128]{1,0:T(8,128)S(1)} collective-permute-done((f32[320,128]{1,0:T(8,128)}, f32[320,128]{1,0:T(8,128)S(1)}, u32[]{:S(2)}, u32[]{:S(2)}) %collective-permute-start.1) | collective-permute-done | bytes 163872 | tf_op jit(solution)/shard_map/ppermute | solution.py:392
  13.1 0.0 copy-start.1
  13.1 0.0 copy-done
  13.1 0.7 %copy-done.1 = f32[320,128]{1,0:T(8,128)} copy-done((f32[320,128]{1,0:T(8,128)}, f32[320,128]{1,0:T(8,128)S(1)}, u32[]{:S(2)}) %copy-start.1) | copy-done | bytes 163864
  13.8 2.7 %edges.1 = (f32[12,3,8,128]{3,2,1,0:T(8,128)}, f32[2,3,8,128]{3,2,1,0:T(8,128)}, f32[2,24,8,128]{3,2,1,0:T(8,128)}) custom-call(f32[320,128]{1,0:T(8,128)} %copy-done, f32[320,128]{1,0:T(8,128)} %copy-done.1, f32[272,256]{1,0:T(8,128)} %get-tuple-element.11.emis, f32[10,2,8,128]{3,2,1,0:T(8,128)} %get-tuple-element.12.strips_own), custom_call_target="tpu_custom_call" | custom-call | tf_op jit(solution)/shard_map/edges/pallas_call | solution.py:403
  16.5 4.1 %collective-permute-start.3 = (f32[12,3,8,128]{3,2,1,0:T(8,128)}, f32[12,3,8,128]{3,2,1,0:T(8,128)S(1)}, u32[]{:S(2)}, u32[]{:S(2)}) collective-permute-start(f32[12,3,8,128]{3,2,1,0:T(8,128)} %get-tuple-element.13.sent_own), channel_id=1, source_target_pairs={{1,0},{2,1},{3,2},{4,3},{5,4},{6,5},{7,6},{0,7},{9,8},{10,9},{11,1... | collective-permute-start | bytes 442376 | tf_op jit(solution)/shard_map/ppermute | solution.py:414
  20.6 0.0 collective-permute-start.2
  20.6 4.1 %collective-permute-done.3.from_high = f32[12,3,8,128]{3,2,1,0:T(8,128)S(1)} collective-permute-done((f32[12,3,8,128]{3,2,1,0:T(8,128)}, f32[12,3,8,128]{3,2,1,0:T(8,128)S(1)}, u32[]{:S(2)}, u32[]{:S(2)}) %collective-permute-start.3) | collective-permute-done | bytes 147488 | tf_op jit(solution)/shard_map/ppermute | solution.py:414
  24.7 0.0 copy-start.2
  24.7 4.8 %collective-permute-done.2.from_low = f32[12,3,8,128]{3,2,1,0:T(8,128)S(1)} collective-permute-done((f32[12,3,8,128]{3,2,1,0:T(8,128)}, f32[12,3,8,128]{3,2,1,0:T(8,128)S(1)}, u32[]{:S(2)}, u32[]{:S(2)}) %collective-permute-start.2) | collective-permute-done | bytes 147488 | tf_op jit(solution)/shard_map/ppermute | solution.py:413
  29.5 0.0 copy-start.3
  29.5 0.0 copy-done.2
  29.5 0.7 %copy-done.3 = f32[12,3,8,128]{3,2,1,0:T(8,128)} copy-done((f32[12,3,8,128]{3,2,1,0:T(8,128)}, f32[12,3,8,128]{3,2,1,0:T(8,128)S(1)}, u32[]{:S(2)}) %copy-start.3) | copy-done | bytes 147480
  30.2 6.5 %substeps.1 = (f32[2,4,8,16,128]{4,3,2,1,0:T(8,128)}, f32[8,16,128]{2,1,0:T(8,128)}) custom-call(f32[2,4,8,16,128]{4,3,2,1,0:T(8,128)} %rad.5, f32[8,16,128]{2,1,0:T(8,128)} %ion.5, f32[8,16,128]{2,1,0:T(8,128)} %den.5, f32[320,128]{1,0:T(8,128)} %copy-done, f32[320,128]{1,0:T(8,128)} %copy-done.1, f32[12,3,8,128]{3,2,1,0:T(8,128)} %get-tuple-element.13.sent_own, ...), custom_call_target="tpu_custom_call" | custom-call | tf_op jit(solution)/shard_map/substeps/pallas_call | solution.py:418
Async XLA Ops:
  1.3 1.3 %copy-start.4 = (f32[1,1,3,256]{3,1,2,0:T(1,128)S(1)}, f32[1,1,3,256]{3,1,2,0:T(1,128)}, u32[]{:S(2)}) copy-start(f32[1,1,3,256]{3,1,2,0:T(1,128)} %param.12) | copy-start | bytes 9220
  5.2 5.6 %collective-permute-start = (f32[320,128]{1,0:T(8,128)}, f32[320,128]{1,0:T(8,128)S(1)}, u32[]{:S(2)}, u32[]{:S(2)}) collective-permute-start(f32[320,128]{1,0:T(8,128)} %get-tuple-element.9), channel_id=1, source_target_pairs={{0,8},{8,0},{16,24},{24,16},{1,9},{9,1},{17,25},{25,17},{2,10},{10... | collective-permute-start | bytes 491528 | tf_op jit(solution)/shard_map/ppermute | solution.py:391
  5.7 7.4 %collective-permute-start.1 = (f32[320,128]{1,0:T(8,128)}, f32[320,128]{1,0:T(8,128)S(1)}, u32[]{:S(2)}, u32[]{:S(2)}) collective-permute-start(f32[320,128]{1,0:T(8,128)} %get-tuple-element.10), channel_id=1, source_target_pairs={{0,24},{8,16},{16,8},{24,0},{1,25},{9,17},{17,9},{25,1},{2,26},{10... | collective-permute-start | bytes 491528 | tf_op jit(solution)/shard_map/ppermute | solution.py:392
  10.9 2.3 %copy-start = (f32[320,128]{1,0:T(8,128)}, f32[320,128]{1,0:T(8,128)S(1)}, u32[]{:S(2)}) copy-start(f32[320,128]{1,0:T(8,128)S(1)} %collective-permute-done.from0) | copy-start | bytes 491524
  13.1 0.7 %copy-start.1 = (f32[320,128]{1,0:T(8,128)}, f32[320,128]{1,0:T(8,128)S(1)}, u32[]{:S(2)}) copy-start(f32[320,128]{1,0:T(8,128)S(1)} %collective-permute-done.1.from1) | copy-start | bytes 491524
  16.5 8.2 %collective-permute-start.3 = (f32[12,3,8,128]{3,2,1,0:T(8,128)}, f32[12,3,8,128]{3,2,1,0:T(8,128)S(1)}, u32[]{:S(2)}, u32[]{:S(2)}) collective-permute-start(f32[12,3,8,128]{3,2,1,0:T(8,128)} %get-tuple-element.13.sent_own), channel_id=1, source_target_pairs={{1,0},{2,1},{3,2},{4,3},{5,4},{6,5},{7,6},{0,7},{9,8},{10,9},{11,1... | collective-permute-start | bytes 442376 | tf_op jit(solution)/shard_map/ppermute | solution.py:414
  20.6 8.9 %collective-permute-start.2 = (f32[12,3,8,128]{3,2,1,0:T(8,128)}, f32[12,3,8,128]{3,2,1,0:T(8,128)S(1)}, u32[]{:S(2)}, u32[]{:S(2)}) collective-permute-start(f32[12,3,8,128]{3,2,1,0:T(8,128)} %get-tuple-element.13.sent_own), channel_id=1, source_target_pairs={{0,1},{1,2},{2,3},{3,4},{4,5},{5,6},{6,7},{7,0},{8,9},{9,10},{10,1... | collective-permute-start | bytes 442376 | tf_op jit(solution)/shard_map/ppermute | solution.py:413
  24.7 4.8 %copy-start.2 = (f32[12,3,8,128]{3,2,1,0:T(8,128)}, f32[12,3,8,128]{3,2,1,0:T(8,128)S(1)}, u32[]{:S(2)}) copy-start(f32[12,3,8,128]{3,2,1,0:T(8,128)S(1)} %collective-permute-done.3.from_high) | copy-start | bytes 442372
  29.5 0.7 %copy-start.3 = (f32[12,3,8,128]{3,2,1,0:T(8,128)}, f32[12,3,8,128]{3,2,1,0:T(8,128)S(1)}, u32[]{:S(2)}) copy-start(f32[12,3,8,128]{3,2,1,0:T(8,128)S(1)} %collective-permute-done.2.from_low) | copy-start | bytes 442372

commit v2 on v1

v2 whole, which is shorter than its diff:
```python
import jax
import jax.numpy as jnp
from jax import lax
from jax.experimental import pallas as pl
from jax.experimental.pallas import tpu as pltpu
from jax.sharding import PartitionSpec as P

SUBSTEPS = 4
CHEM_ITERS = 3
DT = 0.3
ALPHA = 0.4
SIGMA = (1.5, 0.5)

HALO = SUBSTEPS
INNER = HALO - 1


def neighbour_pairs(count, parity):
    return [(i, (i + 1) % count if i % 2 == parity else (i - 1) % count) for i in range(count)]


def halo_parts(fields_full, fields_inner, groups):
    inner = fields_full * HALO
    emis = inner + fields_inner * INNER
    return inner, emis, emis + groups * (INNER + 1)


def deposit(stars, rows, depth, width):
    lum, cell, off = stars
    slots = lum[0].shape[1]
    z = lax.broadcasted_iota(jnp.int32, (depth, slots), 0)
    upper = jnp.where(cell[2] + 1 == depth, 0, cell[2] + 1)
    weight_z = jnp.where(z == cell[2], 1.0 - off[2], 0.0) + jnp.where(z == upper, off[2], 0.0)
    y = lax.broadcasted_iota(jnp.int32, (2 * width, slots), 0)
    weight_y = jnp.where(y == cell[1], 1.0 - off[1], 0.0) + jnp.where(y == cell[1] + 1, off[1], 0.0)
    left = []
    for light in lum:
        for x in rows:
            weight_x = jnp.where(cell[0] == x, 1.0 - off[0], 0.0)
            weight_x = weight_x + jnp.where(cell[0] == x - 1, off[0], 0.0)
            left.append(weight_z * (weight_x * light))
    return lax.dot_general(
        jnp.concatenate(left, axis=0),
        weight_y,
        (((1,), (1,)), ((), ())),
        precision=lax.Precision.HIGHEST,
        preferred_element_type=jnp.float32,
    )


def strip_lane():
    return lax.broadcasted_iota(jnp.int32, (8, 128), 1)


def pack_kernel(
    rad_hbm, ion_hbm, den_hbm, lum_hbm, cell_hbm, off_hbm, count_ref,
    low_y, high_y, to0, to1, strips, emis,
    rad, ion, den, lum_ref, cell_ref, off_ref, sem,
):
    even = lax.rem(lax.axis_index("gx"), 2) == 0
    copies = [
        pltpu.make_async_copy(src, dst, sem.at[k])
        for k, (src, dst) in enumerate(
            (
                (lum_hbm, lum_ref),
                (cell_hbm, cell_ref),
                (off_hbm, off_ref),
                (rad_hbm, rad),
                (ion_hbm, ion),
                (den_hbm, den),
            )
        )
    ]
    for copy in copies:
        copy.start()
    groups, comps, depth, rows_x, width = rad.shape
    owned = rows_x // 8
    lane = strip_lane()
    column = lax.rem(lane, 16)
    zero = jnp.zeros((8, 128), jnp.float32)
    for copy in copies[:3]:
        copy.wait()
    slots = lum_ref.shape[3]
    slot = lax.broadcasted_iota(jnp.int32, (1, slots), 1)
    live = (slot < count_ref[0, 0]).astype(jnp.float32)
    stars = (
        [lum_ref[0, 0, g : g + 1, :] * live for g in range(groups)],
        [cell_ref[a] for a in range(3)],
        [off_ref[a] for a in range(3)],
    )
    table = deposit(stars, range(rows_x + 1), depth, width)

    def plane_of(g, x, half):
        start = (g * (rows_x + 1) + x) * depth
        return table[start : start + depth, half * width : (half + 1) * width]

    for copy in copies[3:]:
        copy.wait()
    reads = [(lambda x, g=g, c=c: rad[g, c, :, x, :]) for g in range(groups) for c in range(comps)]
    reads += [lambda x: ion[:, x, :], lambda x: den[:, x, :]]
    fields = len(reads)
    packs_low = [[zero] * owned for _ in range((fields + groups) // 4)]
    packs_high = [[zero] * owned for _ in range((fields + groups) // 4)]
    tail_low, tail_high = zero, zero

    def add(pack, k, part, source):
        return jnp.where((column >= 4 * k) & (column < 4 * k + 4), pltpu.roll(part, (4 * k - source) % 128, 1), pack)

    for f, read in enumerate(reads):
        for v in range(owned):
            acc = zero
            for group in range(8):
                plane = read(8 * v + group)
                low = pltpu.roll(plane, (16 * group + 4) % 128, 1)
                high = pltpu.roll(plane, (16 * group + 12) % 128, 1)
                at = lane - 16 * group
                acc = jnp.where((at >= 0) & (at < 8), low, jnp.where((at >= 8) & (at < 16), high, acc))
            strips[f, v] = acc
            p, k = f // 4, f % 4
            packs_high[p][v] = add(packs_high[p][v], k, acc, 8)
            packs_low[p][v] = add(packs_low[p][v], k, acc, 4)
    for g in range(groups):
        f = fields + g
        p, k = f // 4, f % 4
        sent, own = [zero] * (owned + 1), [zero] * (owned + 1)
        for x in range(rows_x + 1):
            v, group = x // 8, x % 8
            plane, past = plane_of(g, x, 0), plane_of(g, x, 1)
            emis[g, x] = plane
            low = pltpu.roll(plane, (16 * group + 4) % 128, 1)
            high = pltpu.roll(plane, (16 * group + 12) % 128, 1)
            past_low = pltpu.roll(past, (16 * group + 4) % 128, 1)
            past_high = pltpu.roll(past, (16 * group + 12) % 128, 1)
            at = lane - 16 * group
            s = jnp.where((at >= 4) & (at < 8), low, sent[v])
            s = jnp.where((at >= 8) & (at < 12), high, s)
            sent[v] = jnp.where(at == 12, past_high, s)
            o = jnp.where((at >= 0) & (at < 4), low, own[v])
            o = jnp.where((at >= 12) & (at < 16), high, o)
            own[v] = jnp.where(at == 4, past_low, o)
        for v in range(owned + 1):
            strips[f, v] = own[v]
        for v in range(owned):
            packs_high[p][v] = add(packs_high[p][v], k, sent[v], 9)
            packs_low[p][v] = add(packs_low[p][v], k, sent[v], 4)
        tail_high = add(tail_high, k, sent[owned], 9)
        tail_low = add(tail_low, k, sent[owned], 4)
    for p in range(len(packs_low)):
        for v in range(owned):
            high_y[p * owned + v] = packs_high[p][v]
            low_y[p * owned + v] = packs_low[p][v]
    high_y[len(packs_low) * owned] = tail_high
    low_y[len(packs_low) * owned] = tail_low

    at = 0

    def put(high, low):
        nonlocal at
        to0[at] = jnp.where(even, high, low)
        to1[at] = jnp.where(even, low, high)
        at += 1

    for g in range(groups):
        for c in range(comps):
            for i in range(HALO):
                put(rad[g, c, :, rows_x - HALO + i, :], rad[g, c, :, i, :])
    for ref in (ion, den):
        for i in range(INNER):
            put(ref[:, rows_x - INNER + i, :], ref[:, i, :])
    for g in range(groups):
        for i in range(INNER + 1):
            put(plane_of(g, rows_x - INNER + i, 0), plane_of(g, i, 0))


def edge_kernel(strips, from_low, from_high, joined, to0, to1):
    even = lax.rem(lax.axis_index("gx"), 2) == 0
    fields, tiles, depth, width = strips.shape
    owned = tiles - 1
    groups = len(SIGMA)
    lane = strip_lane()
    column = lax.rem(lane, 16)
    is_right = (column >= 4) & (column < 8)
    is_left = (column >= 8) & (column < 12)
    is_left_e = (column >= 9) & (column < 13)
    done = {}
    for f in range(fields):
        emission = f >= fields - groups
        p, k = f // 4, f % 4
        for v in range(tiles if emission else owned):
            at = p * owned + v
            right = pltpu.roll(from_high[at], (4 - 4 * k) % 128, 1)
            if emission:
                left = pltpu.roll(from_low[at], (9 - 4 * k) % 128, 1)
                value = strips[f, v] + jnp.where(is_right, right, 0.0) + jnp.where(is_left_e, left, 0.0)
            else:
                left = pltpu.roll(from_low[at], (8 - 4 * k) % 128, 1)
                value = jnp.where(is_right, right, jnp.where(is_left, left, strips[f, v]))
            joined[f, v] = value
            done[f, v] = value
    half = width // 2
    for p in range(fields // 2):
        a, b = 2 * p, 2 * p + 1
        high = jnp.where(lane >= half, done[a, owned - 1], pltpu.roll(done[b, owned - 1], half, 1))
        low = jnp.where(lane < half, done[a, 0], pltpu.roll(done[b, 0], half, 1))
        to0[p] = jnp.where(even, high, low)
        to1[p] = jnp.where(even, low, high)
    tail = jnp.zeros((8, 128), jnp.float32)
    for g in range(groups):
        moved = pltpu.roll(done[fields - groups + g, owned], 16 * g, 1) if g else done[fields - groups, owned]
        tail = jnp.where((lane >= 16 * g) & (lane < 16 * g + 16), moved, tail)
    to0[fields // 2] = tail
    to1[fields // 2] = tail


def closure(state):
    photons, flux = state[0], state[1:]
    inverse = 1.0 / photons
    unit = [f * inverse for f in flux]
    fsq = jnp.minimum(unit[0] * unit[0] + unit[1] * unit[1] + unit[2] * unit[2], 1.0)
    square = 4.0 - 3.0 * fsq
    root = square * lax.rsqrt(square)
    shape_term = 3.0 / (2.0 + root)
    diag = (root - 1.0) * (photons * (1.0 / 3.0))
    scaled = [f * shape_term for f in flux]
    xx, yy, zz = (scaled[a] * unit[a] + diag for a in range(3))
    xy, xz, yz = scaled[0] * unit[1], scaled[0] * unit[2], scaled[1] * unit[2]
    return ((flux[0], xx, xy, xz), (flux[1], xy, yy, yz), (flux[2], xz, yz, zz))


def chemistry(state, ion, dens):
    groups = len(state)
    reach = DT * dens
    loss = ALPHA * reach
    push = [state[g][0] * (DT * SIGMA[g]) for g in range(groups)]
    frac = ion
    for step in range(CHEM_ITERS):
        free = reach * (1.0 - frac)
        atten = [1.0 / (1.0 + SIGMA[g] * free) for g in range(groups)]
        gamma = sum((push[g] * atten[g] for g in range(1, groups)), push[0] * atten[0])
        frac = (ion + gamma) / (1.0 + (gamma + loss * frac))
    return [[u * atten[g] for u in state[g]] for g in range(groups)], frac


def step_kernel(
    rad, ion, den, from0, from1, joined, corner0, corner1, emis,
    rad_out, ion_out, u_ref, ion_ref, den_ref, s_ref, e_ref, t_ref,
):
    even = lax.rem(lax.axis_index("gx"), 2) == 0
    groups, comps, depth, rows_x, width = rad.shape
    tiles = joined.shape[1]
    owned = tiles - 1
    cycle = 8 * tiles
    fields = groups * comps
    inner_at, emis_at, _ = halo_parts(fields, 2, groups)
    lane = strip_lane()
    column = lax.rem(lane, 16)

    def beside(at, first=from0, second=from1):
        a, b = first[at], second[at]
        return jnp.where(even, b, a), jnp.where(even, a, b)

    for g in range(groups):
        for c in range(comps):
            f = g * comps + c
            for x in range(rows_x):
                u_ref[f, x + HALO] = rad[g, c, :, x, :]
            for i in range(HALO):
                below, above = beside(f * HALO + i)
                u_ref[f, i] = below
                u_ref[f, rows_x + HALO + i] = above
    for k, (src, dst) in enumerate(((ion, ion_ref), (den, den_ref))):
        for x in range(rows_x):
            dst[x + HALO] = src[:, x, :]
        for i in range(INNER):
            below, above = beside(inner_at + k * INNER + i)
            dst[i + 1] = below
            dst[rows_x + HALO + i] = above

    half = width // 2
    strip_fields = fields + 2 + groups
    for p in range(strip_fields // 2):
        below, above = beside(p, corner0, corner1)
        s_ref[2 * p, owned] = jnp.where(lane < half, above, below)
        s_ref[2 * p + 1, owned] = pltpu.roll(jnp.where(lane < half, below, above), half, 1)
        for f in (2 * p, 2 * p + 1):
            for v in range(owned):
                s_ref[f, v] = joined[f, v]
    tail, _ = beside(strip_fields // 2, corner0, corner1)
    for g in range(groups):
        f = fields + 2 + g
        row_16 = pltpu.roll(tail, (-16 * g) % 128, 1) if g else tail
        s_ref[f, 0] = (s_ref[f, 0] + jnp.where(lane < 16, row_16, 0.0)) * DT
        for v in range(1, owned):
            s_ref[f, v] = s_ref[f, v] * DT
        s_ref[f, owned] = (s_ref[f, owned] + joined[f, owned]) * DT
        for x in range(-INNER, rows_x + INNER):
            parts = []
            if 0 <= x <= rows_x:
                parts.append(emis[g, x])
            if x <= 0:
                parts.append(beside(emis_at + g * (INNER + 1) + x + INNER)[0])
            if x >= rows_x:
                parts.append(beside(emis_at + g * (INNER + 1) + x - rows_x)[1])
            total = sum(parts[1:], parts[0])
            row = x % cycle
            v, group = row // 8, row % 8
            edge = pltpu.roll(s_ref[f, v], (116 - 16 * group) % 128, 1)
            e_ref[g, x + HALO] = jnp.where(lane == 0, edge, total * DT)

    keep, share = 1.0 - 3.0 * DT, 0.5 * DT
    for step in range(SUBSTEPS):
        states = [
            [[s_ref[g * comps + c, v] for c in range(comps)] for g in range(groups)]
            for v in range(tiles)
        ]
        phys = [[closure(states[v][g]) for g in range(groups)] for v in range(tiles)]
        for v in range(tiles):
            for g in range(groups):
                for c in range(comps):
                    u, f = states[v][g][c], phys[v][g][1][c]
                    t_ref[g * comps + c, v] = jnp.where(
                        column == 11, u + f, pltpu.roll(u - f, 6, 1)
                    )
        if step < SUBSTEPS - 1:
            for v in range(tiles):
                new = []
                for g in range(groups):
                    comp = []
                    for c in range(comps):
                        u = states[v][g][c]
                        fx, fy, fz = (phys[v][g][a][c] for a in range(3))
                        vn, vp = (v + 1) % tiles, (v - 1) % tiles
                        down, here_d = states[vn][g][c] - phys[vn][g][0][c], u - fx
                        up, here_u = states[vp][g][c] + phys[vp][g][0][c], u + fx
                        total = jnp.where(
                            lane < 112, pltpu.roll(here_d, 112, 1), pltpu.roll(down, 112, 1)
                        )
                        total = total + jnp.where(
                            lane < 16, pltpu.roll(up, 16, 1), pltpu.roll(here_u, 16, 1)
                        )
                        total = total + pltpu.roll(u - fy, 127, 1) + pltpu.roll(u + fy, 1, 1)
                        total = total + pltpu.roll(u - fz, depth - 1, 0) + pltpu.roll(u + fz, 1, 0)
                        comp.append(keep * u + share * total)
                    comp[0] = comp[0] + s_ref[fields + 2 + g, v]
                    new.append(comp)
                new, frac = chemistry(new, s_ref[fields, v], s_ref[fields + 1, v])
                for g in range(groups):
                    for c in range(comps):
                        s_ref[g * comps + c, v] = new[g][c]
                s_ref[fields, v] = frac

        reach = SUBSTEPS - 1 - step

        def row_terms(x):
            row = x % cycle
            v, group = row // 8, row % 8
            up, down, rest = [], [], []
            for g in range(groups):
                state = [u_ref[g * comps + c, x + HALO] for c in range(comps)]
                px, py, pz = closure(state)
                for c in range(comps):
                    u = state[c]
                    up.append(u + px[c])
                    down.append(u - px[c])
                    if -reach <= x < rows_x + reach:
                        edge = pltpu.roll(t_ref[g * comps + c, v], (117 - 16 * group) % 128, 1)
                        total = jnp.where(lane == width - 1, edge, pltpu.roll(u - py[c], width - 1, 1))
                        total = total + jnp.where(lane == 0, edge, pltpu.roll(u + py[c], 1, 1))
                        total = total + pltpu.roll(u - pz[c], depth - 1, 0)
                        total = total + pltpu.roll(u + pz[c], 1, 0)
                        rest.append(keep * u + share * total)
            return up, down, rest

        before, _, _ = row_terms(-reach - 1)
        here, _, rest = row_terms(-reach)
        for x in range(-reach, rows_x + reach):
            after, down, rest_after = row_terms(x + 1)
            new = []
            for g in range(groups):
                comp = []
                for c in range(comps):
                    k = g * comps + c
                    comp.append(rest[k] + share * (before[k] + down[k]))
                comp[0] = comp[0] + e_ref[g, x + HALO]
                new.append(comp)
            new, frac = chemistry(new, ion_ref[x + HALO], den_ref[x + HALO])
            last = step == SUBSTEPS - 1
            for g in range(groups):
                for c in range(comps):
                    if last:
                        rad_out[g, c, :, x, :] = new[g][c]
                    else:
                        u_ref[g * comps + c, x + HALO] = new[g][c]
            if last:
                ion_out[:, x, :] = frac
            else:
                ion_ref[x + HALO] = frac
            before, here, rest = here, after, rest_after


def on_device(radiation, ion_fraction, density, star_lum, star_cell, star_offset, star_count):
    groups, comps, depth, rows_x, width = radiation.shape
    slots = star_lum.shape[3]
    fields = groups * comps
    strip_fields = fields + 2 + groups
    nx, ny = lax.axis_size("gx"), lax.axis_size("gy")
    if depth != 8 or width != 128 or rows_x % 8 or groups != len(SIGMA) or strip_fields % 4:
        raise ValueError("tile shape")
    if nx % 2:
        raise ValueError("odd axis")
    owned = rows_x // 8
    tiles = owned + 1
    f32 = jnp.float32
    plane = (depth, width)
    rows = rows_x + 2 * HALO
    planes = halo_parts(fields, 2, groups)[2]
    vmem = pl.BlockSpec(memory_space=pltpu.VMEM)
    smem = pl.BlockSpec(memory_space=pltpu.SMEM)
    hbm = pl.BlockSpec(memory_space=pltpu.HBM)
    small = pltpu.CompilerParams(vmem_limit_bytes=8 * 1024 * 1024)

    def out(*shape):
        return jax.ShapeDtypeStruct(shape + plane, f32)

    star_cell = star_cell.reshape(3, 1, slots)
    star_offset = star_offset.reshape(3, 1, slots)
    arrays = (radiation, ion_fraction, density, star_lum, star_cell, star_offset)
    sent = strip_fields // 4 * owned + 1
    low_y, high_y, to0, to1, strips, emis = pl.pallas_call(
        pack_kernel,
        out_shape=[
            out(sent), out(sent), out(planes), out(planes), out(strip_fields, tiles), out(groups, rows_x + 1)
        ],
        in_specs=[hbm] * 6 + [smem],
        scratch_shapes=[pltpu.VMEM(a.shape, a.dtype) for a in arrays] + [pltpu.SemaphoreType.DMA((6,))],
        compiler_params=small,
        name="pack",
    )(*[pltpu.with_memory_space_constraint(a, pltpu.HBM) for a in arrays], star_count)
    up = [(i, (i + 1) % ny) for i in range(ny)]
    down = [((i + 1) % ny, i) for i in range(ny)]
    from_low = lax.ppermute(high_y, "gy", up)
    from_high = lax.ppermute(low_y, "gy", down)
    from0 = lax.ppermute(to0, "gx", neighbour_pairs(nx, 0))
    from1 = lax.ppermute(to1, "gx", neighbour_pairs(nx, 1))
    joined, edge0, edge1 = pl.pallas_call(
        edge_kernel,
        out_shape=[out(strip_fields, tiles), out(strip_fields // 2 + 1), out(strip_fields // 2 + 1)],
        in_specs=[vmem] * 3,
        compiler_params=small,
        name="edges",
    )(strips, from_low, from_high)
    corner0 = lax.ppermute(edge0, "gx", neighbour_pairs(nx, 0))
    corner1 = lax.ppermute(edge1, "gx", neighbour_pairs(nx, 1))
    return tuple(
        pl.pallas_call(
            step_kernel,
            out_shape=[
                jax.ShapeDtypeStruct(radiation.shape, f32),
                jax.ShapeDtypeStruct(ion_fraction.shape, f32),
            ],
            in_specs=[vmem] * 9,
            scratch_shapes=[
                pltpu.VMEM((fields, rows) + plane, f32),
                pltpu.VMEM((rows,) + plane, f32),
                pltpu.VMEM((rows,) + plane, f32),
                pltpu.VMEM((strip_fields, tiles) + plane, f32),
                pltpu.VMEM((groups, rows) + plane, f32),
                pltpu.VMEM((fields, tiles) + plane, f32),
            ],
            compiler_params=small,
            name="substeps",
        )(radiation, ion_fraction, density, from0, from1, joined, corner0, corner1, emis)
    )


def solution(mesh):
    return jax.shard_map(
        on_device,
        mesh=mesh,
        in_specs=(
            P(None, None, None, "gx", "gy"),
            P(None, "gx", "gy"),
            P(None, "gx", "gy"),
            P("gx", "gy", None, None),
            P("gx", "gy", None, None),
            P("gx", "gy", None, None),
            P("gx", "gy"),
        ),
        out_specs=(P(None, None, None, "gx", "gy"), P(None, "gx", "gy")),
        check_vma=False,
    )
```

time: 36.9 us -> 23.3 us (0.63)
  waiting for transfers between devices: 11.1 us -> 4.8 us
  Pallas kernels: 13.8 us -> 8.58 us
  local copies, waits for them, and re-layouts: 3.2 us -> 0.01 us
  starting transfers between devices: 7.25 us -> 8.39 us
    ppermute x2 -> x4, waiting for transfers between devices: 8.89 us -> 4.79 us  [the longest x1 2.17 us: on_device(): corner1 = lax.ppermute(edge1, 'gx', neighbour_pairs(nx, 1))]
    pallas_call x3 -> x2, Pallas kernels: 7.29 us -> 3.45 us  [the longest x1 3.29 us: on_device(): pl.pallas_call(pack_kernel, out_shape=[out(sent), out(sent), out(planes),...]
    unnamed x12 -> x6, local copies, waits for them, and re-layouts: 3.2 us -> 0.01 us
    ppermute x1, waiting for transfers between devices: 2.26 us -> 0.01 us  [on_device(): from1 = lax.ppermute(to1, 'gx', neighbour_pairs(nx, 1))]
    pallas_call x1, Pallas kernels: 6.48 us -> 5.12 us  [on_device(): pl.pallas_call(step_kernel, out_shape=[jax.ShapeDtypeStruct(radiation.sha...]
    ppermute x2 -> x4, starting transfers between devices: 4.14 us -> 5.21 us  [the longest x1 3.23 us: on_device(): from_high = lax.ppermute(low_y, 'gy', down)]
  transfers between devices with their start and end apart: 4 -> 6, of which waited for: 3 -> 3; matrix products, arithmetic and copies ran while one was open for 0% -> 0% of each run, Pallas kernels for 7% -> 1%
where the time goes in v2:
time: 23.3 us; the launch traced here: 23.2 us
  Pallas kernels  8.58 us (37%)
  starting transfers between devices  8.39 us (36%)
  waiting for transfers between devices  4.8 us (21%)
  between operations  1.39 us (6%)
    pallas_call x1, Pallas kernels, on_device(): pl.pallas_call(step_kernel, out_shape=[jax.ShapeDtypeStruct(radiation.sha...  5.12 us
    pallas_call x1, Pallas kernels, on_device(): pl.pallas_call(pack_kernel, out_shape=[out(sent), out(sent), out(planes),...  3.29 us
    ppermute x1, starting transfers between devices, on_device(): from_high = lax.ppermute(low_y, 'gy', down)  3.23 us
    ppermute x1, starting transfers between devices, on_device(): from1 = lax.ppermute(to1, 'gx', neighbour_pairs(nx, 1))  2.62 us
    ppermute x1, waiting for transfers between devices, on_device(): corner1 = lax.ppermute(edge1, 'gx', neighbour_pairs(nx, 1))  2.17 us
    ppermute x1, waiting for transfers between devices, on_device(): from_low = lax.ppermute(high_y, 'gy', up)  1.84 us
    ppermute x1, starting transfers between devices, on_device(): from_low = lax.ppermute(high_y, 'gy', up)  1.49 us
    ppermute x1, waiting for transfers between devices, on_device(): corner0 = lax.ppermute(edge0, 'gx', neighbour_pairs(nx, 0))  0.77 us
  transfers between devices with their start and end apart: 6, of which 3 were waited for; matrix products, arithmetic and copies ran while one was open for 0% of the time, Pallas kernels for 1%

profile of v2, /device:TPU:0, one launch (start us, length us, event | category | flops | bytes accessed | tf_op | source)
XLA Modules:
  0.0 23.2 jit_solution(2621750639766591908)
XLA Ops:
  0.6 0.0 copy-start
  1.3 3.3 %pack.1 = (f32[7,8,128]{2,1,0:T(8,128)S(1)}, f32[7,8,128]{2,1,0:T(8,128)S(1)}, f32[46,8,128]{2,1,0:T(8,128)S(1)}, f32[46,8,128]{2,1,0:T(8,128)S(1)}, f32[12,3,8,...) custom-call(f32[2,4,8,16,128]{4,3,2,1,0:T(8,128)} %rad.1, f32[8,16,128]{2,1,0:T(8,128)} %ion.1, f32[8,16,128]{2,1,0:T(8,128)} %den.1, ...), custom_call_target="tpu_custom_call" | custom-call | tf_op jit(solution)/shard_map/pack/pallas_call | solution.py:429
  4.6 0.6 %collective-permute-start = (f32[46,8,128]{2,1,0:T(8,128)S(1)}, f32[46,8,128]{2,1,0:T(8,128)S(1)}, u32[]{:S(2)}, u32[]{:S(2)}) collective-permute-start(f32[46,8,128]{2,1,0:T(8,128)S(1)} %get-tuple-element.11), channel_id=1, source_target_pairs={{0,8},{8,0},{16,24},{24,16},{1,9},{9,1},{17,25},{25,17},{2,10},{10... | collective-permute-start | bytes 565256 | tf_op jit(solution)/shard_map/ppermute | solution.py:443
  5.2 2.6 %collective-permute-start.1 = (f32[46,8,128]{2,1,0:T(8,128)S(1)}, f32[46,8,128]{2,1,0:T(8,128)S(1)}, u32[]{:S(2)}, u32[]{:S(2)}) collective-permute-start(f32[46,8,128]{2,1,0:T(8,128)S(1)} %get-tuple-element.12), channel_id=1, source_target_pairs={{0,24},{8,16},{16,8},{24,0},{1,25},{9,17},{17,9},{25,1},{2,26},{10... | collective-permute-start | bytes 565256 | tf_op jit(solution)/shard_map/ppermute | solution.py:444
  7.8 1.5 %collective-permute-start.2 = (f32[7,8,128]{2,1,0:T(8,128)S(1)}, f32[7,8,128]{2,1,0:T(8,128)S(1)}, u32[]{:S(2)}, u32[]{:S(2)}) collective-permute-start(f32[7,8,128]{2,1,0:T(8,128)S(1)} %get-tuple-element.14), channel_id=1, source_target_pairs={{0,1},{1,2},{2,3},{3,4},{4,5},{5,6},{6,7},{7,0},{8,9},{9,10},{10,1... | collective-permute-start | bytes 86024 | tf_op jit(solution)/shard_map/ppermute | solution.py:441
  9.3 3.2 %collective-permute-start.3 = (f32[7,8,128]{2,1,0:T(8,128)S(1)}, f32[7,8,128]{2,1,0:T(8,128)S(1)}, u32[]{:S(2)}, u32[]{:S(2)}) collective-permute-start(f32[7,8,128]{2,1,0:T(8,128)S(1)} %get-tuple-element.15), channel_id=1, source_target_pairs={{1,0},{2,1},{3,2},{4,3},{5,4},{6,5},{7,6},{0,7},{9,8},{10,9},{11,1... | collective-permute-start | bytes 86024 | tf_op jit(solution)/shard_map/ppermute | solution.py:442
  12.5 1.8 %collective-permute-done.2.from_low = f32[7,8,128]{2,1,0:T(8,128)S(1)} collective-permute-done((f32[7,8,128]{2,1,0:T(8,128)S(1)}, f32[7,8,128]{2,1,0:T(8,128)S(1)}, u32[]{:S(2)}, u32[]{:S(2)}) %collective-permute-start.2) | collective-permute-done | bytes 28704 | tf_op jit(solution)/shard_map/ppermute | solution.py:441
  14.4 0.0 collective-permute-done.3.from_high
  14.4 0.0 copy-start.1
  14.4 0.0 copy-start.2
  14.4 0.2 edges.1
  14.6 0.1 collective-permute-start.4
  14.6 0.4 %collective-permute-start.5 = (f32[7,8,128]{2,1,0:T(8,128)S(1)}, f32[7,8,128]{2,1,0:T(8,128)S(1)}, u32[]{:S(2)}, u32[]{:S(2)}) collective-permute-start(f32[7,8,128]{2,1,0:T(8,128)S(1)} %get-tuple-element.18), channel_id=1, source_target_pairs={{0,24},{8,16},{16,8},{24,0},{1,25},{9,17},{17,9},{25,1},{2,26},{10... | collective-permute-start | bytes 86024 | tf_op jit(solution)/shard_map/ppermute | solution.py:453
  15.1 0.8 %collective-permute-done.4.corner0 = f32[7,8,128]{2,1,0:T(8,128)S(1)} collective-permute-done((f32[7,8,128]{2,1,0:T(8,128)S(1)}, f32[7,8,128]{2,1,0:T(8,128)S(1)}, u32[]{:S(2)}, u32[]{:S(2)}) %collective-permute-start.4) | collective-permute-done | bytes 28704 | tf_op jit(solution)/shard_map/ppermute | solution.py:452
  15.8 2.2 %collective-permute-done.5.corner1 = f32[7,8,128]{2,1,0:T(8,128)S(1)} collective-permute-done((f32[7,8,128]{2,1,0:T(8,128)S(1)}, f32[7,8,128]{2,1,0:T(8,128)S(1)}, u32[]{:S(2)}, u32[]{:S(2)}) %collective-permute-start.5) | collective-permute-done | bytes 28704 | tf_op jit(solution)/shard_map/ppermute | solution.py:453
  18.0 0.0 collective-permute-done.from0
  18.0 0.0 collective-permute-done.1.from1
  18.0 0.0 copy-done
  18.0 0.0 copy-done.1
  18.0 0.0 copy-done.2
  18.0 5.1 %substeps.1 = (f32[2,4,8,16,128]{4,3,2,1,0:T(8,128)}, f32[8,16,128]{2,1,0:T(8,128)}) custom-call(f32[2,4,8,16,128]{4,3,2,1,0:T(8,128)S(1)} %copy-done, f32[8,16,128]{2,1,0:T(8,128)S(1)} %copy-done.1, f32[8,16,128]{2,1,0:T(8,128)S(1)} %copy-done.2, f32[46,8,128]{2,1,0:T(8,128)S(1)} %collective-permute-done.from0, ...), custom_call_target="tpu_custom_call" | custom-call | tf_op jit(solution)/shard_map/substeps/pallas_call | solution.py:455
Async XLA Ops:
  0.6 17.4 %copy-start = (f32[2,4,8,16,128]{4,3,2,1,0:T(8,128)S(1)}, f32[2,4,8,16,128]{4,3,2,1,0:T(8,128)}, u32[]{:S(2)}) copy-start(f32[2,4,8,16,128]{4,3,2,1,0:T(8,128)} %rad.1) | copy-start | bytes 1572868
  4.6 13.4 %collective-permute-start = (f32[46,8,128]{2,1,0:T(8,128)S(1)}, f32[46,8,128]{2,1,0:T(8,128)S(1)}, u32[]{:S(2)}, u32[]{:S(2)}) collective-permute-start(f32[46,8,128]{2,1,0:T(8,128)S(1)} %get-tuple-element.11), channel_id=1, source_target_pairs={{0,8},{8,0},{16,24},{24,16},{1,9},{9,1},{17,25},{25,17},{2,10},{10... | collective-permute-start | bytes 565256 | tf_op jit(solution)/shard_map/ppermute | solution.py:443
  5.2 12.8 %collective-permute-start.1 = (f32[46,8,128]{2,1,0:T(8,128)S(1)}, f32[46,8,128]{2,1,0:T(8,128)S(1)}, u32[]{:S(2)}, u32[]{:S(2)}) collective-permute-start(f32[46,8,128]{2,1,0:T(8,128)S(1)} %get-tuple-element.12), channel_id=1, source_target_pairs={{0,24},{8,16},{16,8},{24,0},{1,25},{9,17},{17,9},{25,1},{2,26},{10... | collective-permute-start | bytes 565256 | tf_op jit(solution)/shard_map/ppermute | solution.py:444
  7.8 6.6 %collective-permute-start.2 = (f32[7,8,128]{2,1,0:T(8,128)S(1)}, f32[7,8,128]{2,1,0:T(8,128)S(1)}, u32[]{:S(2)}, u32[]{:S(2)}) collective-permute-start(f32[7,8,128]{2,1,0:T(8,128)S(1)} %get-tuple-element.14), channel_id=1, source_target_pairs={{0,1},{1,2},{2,3},{3,4},{4,5},{5,6},{6,7},{7,0},{8,9},{9,10},{10,1... | collective-permute-start | bytes 86024 | tf_op jit(solution)/shard_map/ppermute | solution.py:441
  9.3 5.1 %collective-permute-start.3 = (f32[7,8,128]{2,1,0:T(8,128)S(1)}, f32[7,8,128]{2,1,0:T(8,128)S(1)}, u32[]{:S(2)}, u32[]{:S(2)}) collective-permute-start(f32[7,8,128]{2,1,0:T(8,128)S(1)} %get-tuple-element.15), channel_id=1, source_target_pairs={{1,0},{2,1},{3,2},{4,3},{5,4},{6,5},{7,6},{0,7},{9,8},{10,9},{11,1... | collective-permute-start | bytes 86024 | tf_op jit(solution)/shard_map/ppermute | solution.py:442
  14.4 3.6 %copy-start.1 = (f32[8,16,128]{2,1,0:T(8,128)S(1)}, f32[8,16,128]{2,1,0:T(8,128)}, u32[]{:S(2)}) copy-start(f32[8,16,128]{2,1,0:T(8,128)} %ion.1) | copy-start | bytes 196612
  14.4 3.6 %copy-start.2 = (f32[8,16,128]{2,1,0:T(8,128)S(1)}, f32[8,16,128]{2,1,0:T(8,128)}, u32[]{:S(2)}) copy-start(f32[8,16,128]{2,1,0:T(8,128)} %den.1) | copy-start | bytes 196612
  14.6 1.3 %collective-permute-start.4 = (f32[7,8,128]{2,1,0:T(8,128)S(1)}, f32[7,8,128]{2,1,0:T(8,128)S(1)}, u32[]{:S(2)}, u32[]{:S(2)}) collective-permute-start(f32[7,8,128]{2,1,0:T(8,128)S(1)} %get-tuple-element.17), channel_id=1, source_target_pairs={{0,8},{8,0},{16,24},{24,16},{1,9},{9,1},{17,25},{25,17},{2,10},{10... | collective-permute-start | bytes 86024 | tf_op jit(solution)/shard_map/ppermute | solution.py:452
  14.6 3.4 %collective-permute-start.5 = (f32[7,8,128]{2,1,0:T(8,128)S(1)}, f32[7,8,128]{2,1,0:T(8,128)S(1)}, u32[]{:S(2)}, u32[]{:S(2)}) collective-permute-start(f32[7,8,128]{2,1,0:T(8,128)S(1)} %get-tuple-element.18), channel_id=1, source_target_pairs={{0,24},{8,16},{16,8},{24,0},{1,25},{9,17},{17,9},{25,1},{2,26},{10... | collective-permute-start | bytes 86024 | tf_op jit(solution)/shard_map/ppermute | solution.py:453

commit v3 on v2

--- a/solution.py
+++ b/solution.py
@@ -53,9 +53,9 @@
 
 
 def pack_kernel(
-    rad_hbm, ion_hbm, den_hbm, lum_hbm, cell_hbm, off_hbm, count_ref,
+    rad_hbm, ion_hbm, den_hbm, lum_hbm, cell_hbm, off_hbm, count_hbm,
     low_y, high_y, to0, to1, strips, emis,
-    rad, ion, den, lum_ref, cell_ref, off_ref, sem,
+    rad, ion, den, lum_ref, cell_ref, off_ref, count_ref, sem,
 ):
     even = lax.rem(lax.axis_index("gx"), 2) == 0
     copies = [
@@ -65,6 +65,7 @@
                 (lum_hbm, lum_ref),
                 (cell_hbm, cell_ref),
                 (off_hbm, off_ref),
+                (count_hbm, count_ref),
                 (rad_hbm, rad),
                 (ion_hbm, ion),
                 (den_hbm, den),
@@ -78,11 +79,11 @@
     lane = strip_lane()
     column = lax.rem(lane, 16)
     zero = jnp.zeros((8, 128), jnp.float32)
-    for copy in copies[:3]:
+    for copy in copies[:4]:
         copy.wait()
     slots = lum_ref.shape[3]
     slot = lax.broadcasted_iota(jnp.int32, (1, slots), 1)
-    live = (slot < count_ref[0, 0]).astype(jnp.float32)
+    live = (slot < count_ref[...]).astype(jnp.float32)
     stars = (
         [lum_ref[0, 0, g : g + 1, :] * live for g in range(groups)],
         [cell_ref[a] for a in range(3)],
@@ -94,7 +95,7 @@
         start = (g * (rows_x + 1) + x) * depth
         return table[start : start + depth, half * width : (half + 1) * width]
 
-    for copy in copies[3:]:
+    for copy in copies[4:]:
         copy.wait()
     reads = [(lambda x, g=g, c=c: rad[g, c, :, x, :]) for g in range(groups) for c in range(comps)]
     reads += [lambda x: ion[:, x, :], lambda x: den[:, x, :]]
@@ -241,40 +242,158 @@
     return [[u * atten[g] for u in state[g]] for g in range(groups)], frac
 
 
-def step_kernel(
-    rad, ion, den, from0, from1, joined, corner0, corner1, emis,
-    rad_out, ion_out, u_ref, ion_ref, den_ref, s_ref, e_ref, t_ref,
+def strip_step(s_ref, t_ref, tiles, groups, comps, depth, update):
+    fields = groups * comps
+    keep, share = 1.0 - 3.0 * DT, 0.5 * DT
+    lane = strip_lane()
+    column = lax.rem(lane, 16)
+    states = [
+        [[s_ref[g * comps + c, v] for c in range(comps)] for g in range(groups)] for v in range(tiles)
+    ]
+    phys = [[closure(states[v][g]) for g in range(groups)] for v in range(tiles)]
+    for v in range(tiles):
+        for g in range(groups):
+            for c in range(comps):
+                u, f = states[v][g][c], phys[v][g][1][c]
+                t_ref[g * comps + c, v] = jnp.where(column == 11, u + f, pltpu.roll(u - f, 6, 1))
+    if not update:
+        return
+    for v in range(tiles):
+        new = []
+        for g in range(groups):
+            comp = []
+            for c in range(comps):
+                u = states[v][g][c]
+                fx, fy, fz = (phys[v][g][a][c] for a in range(3))
+                vn, vp = (v + 1) % tiles, (v - 1) % tiles
+                down, here_d = states[vn][g][c] - phys[vn][g][0][c], u - fx
+                up, here_u = states[vp][g][c] + phys[vp][g][0][c], u + fx
+                total = pltpu.roll(jnp.where(lane < 16, down, here_d), 112, 1)
+                total = total + pltpu.roll(jnp.where(lane >= 112, up, here_u), 16, 1)
+                total = total + pltpu.roll(u - fy, 127, 1) + pltpu.roll(u + fy, 1, 1)
+                total = total + pltpu.roll(u - fz, depth - 1, 0) + pltpu.roll(u + fz, 1, 0)
+                comp.append(keep * u + share * total)
+            comp[0] = comp[0] + s_ref[fields + 2 + g, v]
+            new.append(comp)
+        new, frac = chemistry(new, s_ref[fields, v], s_ref[fields + 1, v])
+        for g in range(groups):
+            for c in range(comps):
+                s_ref[g * comps + c, v] = new[g][c]
+        s_ref[fields, v] = frac
+
+
+def sweep(lo, hi, read, source, ion_of, den_of, write, t_ref, groups, comps, first_up=None, last_down=None):
+    keep, share = 1.0 - 3.0 * DT, 0.5 * DT
+    lane = strip_lane()
+    depth, width = lane.shape
+    cycle = 8 * t_ref.shape[1]
+
+    def row_terms(x, inside):
+        row = x % cycle
+        v, group = row // 8, row % 8
+        up, down, rest = [], [], []
+        for g in range(groups):
+            state = [read(g * comps + c, x) for c in range(comps)]
+            px, py, pz = closure(state)
+            for c in range(comps):
+                u = state[c]
+                up.append(u + px[c])
+                down.append(u - px[c])
+                if inside:
+                    edge = pltpu.roll(t_ref[g * comps + c, v], (117 - 16 * group) % 128, 1)
+                    total = jnp.where(lane == width - 1, edge, pltpu.roll(u - py[c], width - 1, 1))
+                    total = total + jnp.where(lane == 0, edge, pltpu.roll(u + py[c], 1, 1))
+                    total = total + pltpu.roll(u - pz[c], depth - 1, 0)
+                    total = total + pltpu.roll(u + pz[c], 1, 0)
+                    rest.append(keep * u + share * total)
+        return up, down, rest
+
+    before = row_terms(lo - 1, False)[0] if first_up is None else first_up
+    here, low_down, rest = row_terms(lo, True)
+    for x in range(lo, hi):
+        if x + 1 < hi:
+            after, down, rest_after = row_terms(x + 1, True)
+        else:
+            after, rest_after = None, None
+            down = row_terms(hi, False)[1] if last_down is None else last_down
+        new = []
+        for g in range(groups):
+            comp = []
+            for c in range(comps):
+                k = g * comps + c
+                comp.append(rest[k] + share * (before[k] + down[k]))
+            comp[0] = comp[0] + source(g, x)
+            new.append(comp)
+        new, frac = chemistry(new, ion_of(x), den_of(x))
+        write(x, [new[g][c] for g in range(groups) for c in range(comps)], frac)
+        if x + 1 < hi:
+            before, here, rest = here, after, rest_after
+    return low_down, here
+
+
+def inner_kernel(rad, ion, den, joined, emis, u_ref, ion_ref, saved, s_ref, e_ref, t_ref):
+    groups, comps, depth, rows_x, width = rad.shape
+    tiles = rows_x // 8
+    fields = groups * comps
+    lane = strip_lane()
+    for g in range(groups):
+        for c in range(comps):
+            for x in range(rows_x):
+                u_ref[g * comps + c, x] = rad[g, c, :, x, :]
+    for x in range(rows_x):
+        ion_ref[x] = ion[:, x, :]
+    for f in range(fields + 2):
+        for v in range(tiles):
+            s_ref[f, v] = joined[f, v]
+    for g in range(groups):
+        f = fields + 2 + g
+        for v in range(tiles):
+            s_ref[f, v] = joined[f, v] * DT
+        for x in range(1, rows_x - 1):
+            v, group = x // 8, x % 8
+            edge = pltpu.roll(s_ref[f, v], (116 - 16 * group) % 128, 1)
+            e_ref[g, x] = jnp.where(lane == 0, edge, emis[g, x] * DT)
+
+    def write(x, values, frac):
+        for k, value in enumerate(values):
+            u_ref[k, x] = value
+        ion_ref[x] = frac
+
+    for step in range(SUBSTEPS):
+        strip_step(s_ref, t_ref, tiles, groups, comps, depth, step < SUBSTEPS - 1)
+        down, up = sweep(
+            step + 1,
+            rows_x - 1 - step,
+            lambda k, x: u_ref[k, x],
+            lambda g, x: e_ref[g, x],
+            lambda x: ion_ref[x],
+            lambda x: den[:, x, :],
+            write,
+            t_ref,
+            groups,
+            comps,
+        )
+        for k in range(fields):
+            saved[0, step, k] = down[k]
+            saved[1, step, k] = up[k]
+
+
+def outer_kernel(
+    u_mid, ion_mid, saved, den, from0, from1, joined, corner0, corner1, emis,
+    rad_out, ion_out, u_ref, ion_ref, s_ref, e_ref, t_ref,
 ):
     even = lax.rem(lax.axis_index("gx"), 2) == 0
-    groups, comps, depth, rows_x, width = rad.shape
+    groups, comps, depth, rows_x, width = rad_out.shape
     tiles = joined.shape[1]
     owned = tiles - 1
     cycle = 8 * tiles
     fields = groups * comps
     inner_at, emis_at, _ = halo_parts(fields, 2, groups)
     lane = strip_lane()
-    column = lax.rem(lane, 16)
 
     def beside(at, first=from0, second=from1):
         a, b = first[at], second[at]
         return jnp.where(even, b, a), jnp.where(even, a, b)
-
-    for g in range(groups):
-        for c in range(comps):
-            f = g * comps + c
-            for x in range(rows_x):
-                u_ref[f, x + HALO] = rad[g, c, :, x, :]
-            for i in range(HALO):
-                below, above = beside(f * HALO + i)
-                u_ref[f, i] = below
-                u_ref[f, rows_x + HALO + i] = above
-    for k, (src, dst) in enumerate(((ion, ion_ref), (den, den_ref))):
-        for x in range(rows_x):
-            dst[x + HALO] = src[:, x, :]
-        for i in range(INNER):
-            below, above = beside(inner_at + k * INNER + i)
-            dst[i + 1] = below
-            dst[rows_x + HALO + i] = above
 
     half = width // 2
     strip_fields = fields + 2 + groups
@@ -285,6 +404,7 @@
         for f in (2 * p, 2 * p + 1):
             for v in range(owned):
                 s_ref[f, v] = joined[f, v]
+    edge_rows = list(range(-INNER, HALO)) + list(range(rows_x - HALO, rows_x + INNER))
     tail, _ = beside(strip_fields // 2, corner0, corner1)
     for g in range(groups):
         f = fields + 2 + g
@@ -293,7 +413,7 @@
         for v in range(1, owned):
             s_ref[f, v] = s_ref[f, v] * DT
         s_ref[f, owned] = (s_ref[f, owned] + joined[f, owned]) * DT
-        for x in range(-INNER, rows_x + INNER):
+        for x in edge_rows:
             parts = []
             if 0 <= x <= rows_x:
                 parts.append(emis[g, x])
@@ -307,95 +427,62 @@
             edge = pltpu.roll(s_ref[f, v], (116 - 16 * group) % 128, 1)
             e_ref[g, x + HALO] = jnp.where(lane == 0, edge, total * DT)
 
-    keep, share = 1.0 - 3.0 * DT, 0.5 * DT
+    for f in range(fields):
+        for i in range(HALO):
+            below, above = beside(f * HALO + i)
+            u_ref[f, i] = below
+            u_ref[f, rows_x + HALO + i] = above
+            u_ref[f, HALO + i] = u_mid[f, i]
+            u_ref[f, rows_x + i] = u_mid[f, rows_x - HALO + i]
+    for i in range(HALO):
+        ion_ref[HALO + i] = ion_mid[i]
+        ion_ref[rows_x + i] = ion_mid[rows_x - HALO + i]
+    for i in range(INNER):
+        below, above = beside(inner_at + i)
+        ion_ref[i + 1] = below
+        ion_ref[rows_x + HALO + i] = above
+
+    def den_of(x):
+        if x < 0:
+            return beside(inner_at + INNER + x + INNER)[0]
+        if x >= rows_x:
+            return beside(inner_at + INNER + x - rows_x)[1]
+        return den[:, x, :]
+
+    def finish(x, values, frac):
+        for k, value in enumerate(values):
+            rad_out[k // comps, k % comps, :, x, :] = value
+        ion_out[:, x, :] = frac
+
+    def write(x, values, frac):
+        for k, value in enumerate(values):
+            u_ref[k, x + HALO] = value
+        ion_ref[x + HALO] = frac
+
+    for x in range(HALO, rows_x - HALO):
+        finish(x, [u_mid[k, x] for k in range(fields)], ion_mid[x])
+
     for step in range(SUBSTEPS):
-        states = [
-            [[s_ref[g * comps + c, v] for c in range(comps)] for g in range(groups)]
-            for v in range(tiles)
-        ]
-        phys = [[closure(states[v][g]) for g in range(groups)] for v in range(tiles)]
-        for v in range(tiles):
-            for g in range(groups):
-                for c in range(comps):
-                    u, f = states[v][g][c], phys[v][g][1][c]
-                    t_ref[g * comps + c, v] = jnp.where(
-                        column == 11, u + f, pltpu.roll(u - f, 6, 1)
-                    )
-        if step < SUBSTEPS - 1:
-            for v in range(tiles):
-                new = []
-                for g in range(groups):
-                    comp = []
-                    for c in range(comps):
-                        u = states[v][g][c]
-                        fx, fy, fz = (phys[v][g][a][c] for a in range(3))
-                        vn, vp = (v + 1) % tiles, (v - 1) % tiles
-                        down, here_d = states[vn][g][c] - phys[vn][g][0][c], u - fx
-                        up, here_u = states[vp][g][c] + phys[vp][g][0][c], u + fx
-                        total = jnp.where(
-                            lane < 112, pltpu.roll(here_d, 112, 1), pltpu.roll(down, 112, 1)
-                        )
-                        total = total + jnp.where(
-                            lane < 16, pltpu.roll(up, 16, 1), pltpu.roll(here_u, 16, 1)
-                        )
-                        total = total + pltpu.roll(u - fy, 127, 1) + pltpu.roll(u + fy, 1, 1)
-                        total = total + pltpu.roll(u - fz, depth - 1, 0) + pltpu.roll(u + fz, 1, 0)
-                        comp.append(keep * u + share * total)
-                    comp[0] = comp[0] + s_ref[fields + 2 + g, v]
-                    new.append(comp)
-                new, frac = chemistry(new, s_ref[fields, v], s_ref[fields + 1, v])
-                for g in range(groups):
-                    for c in range(comps):
-                        s_ref[g * comps + c, v] = new[g][c]
-                s_ref[fields, v] = frac
-
-        reach = SUBSTEPS - 1 - step
-
-        def row_terms(x):
-            row = x % cycle
-            v, group = row // 8, row % 8
-            up, down, rest = [], [], []
-            for g in range(groups):
-                state = [u_ref[g * comps + c, x + HALO] for c in range(comps)]
-                px, py, pz = closure(state)
-                for c in range(comps):
-                    u = state[c]
-                    up.append(u + px[c])
-                    down.append(u - px[c])
-                    if -reach <= x < rows_x + reach:
-                        edge = pltpu.roll(t_ref[g * comps + c, v], (117 - 16 * group) % 128, 1)
-                        total = jnp.where(lane == width - 1, edge, pltpu.roll(u - py[c], width - 1, 1))
-                        total = total + jnp.where(lane == 0, edge, pltpu.roll(u + py[c], 1, 1))
-                        total = total + pltpu.roll(u - pz[c], depth - 1, 0)
-                        total = total + pltpu.roll(u + pz[c], 1, 0)
-                        rest.append(keep * u + share * total)
-            return up, down, rest
-
-        before, _, _ = row_terms(-reach - 1)
-        here, _, rest = row_terms(-reach)
-        for x in range(-reach, rows_x + reach):
-            after, down, rest_after = row_terms(x + 1)
-            new = []
-            for g in range(groups):
-                comp = []
-                for c in range(comps):
-                    k = g * comps + c
-                    comp.append(rest[k] + share * (before[k] + down[k]))
-                comp[0] = comp[0] + e_ref[g, x + HALO]
-                new.append(comp)
-            new, frac = chemistry(new, ion_ref[x + HALO], den_ref[x + HALO])
-            last = step == SUBSTEPS - 1
-            for g in range(groups):
-                for c in range(comps):
-                    if last:
-                        rad_out[g, c, :, x, :] = new[g][c]
-                    else:
-                        u_ref[g * comps + c, x + HALO] = new[g][c]
-            if last:
-                ion_out[:, x, :] = frac
-            else:
-                ion_ref[x + HALO] = frac
-            before, here, rest = here, after, rest_after
+        strip_step(s_ref, t_ref, tiles, groups, comps, depth, step < SUBSTEPS - 1)
+        last = step == SUBSTEPS - 1
+        common = (
+            lambda k, x: u_ref[k, x + HALO],
+            lambda g, x: e_ref[g, x + HALO],
+            lambda x: ion_ref[x + HALO],
+            den_of,
+            finish if last else write,
+            t_ref,
+            groups,
+            comps,
+        )
+        rest = INNER - step
+        sweep(-rest, step + 1, *common, last_down=[saved[0, step, k] for k in range(fields)])
+        sweep(
+            rows_x - 1 - step,
+            rows_x + rest,
+            *common,
+            first_up=[saved[1, step, k] for k in range(fields)],
+        )
 
 
 def on_device(radiation, ion_fraction, density, star_lum, star_cell, star_offset, star_count):
@@ -404,7 +491,7 @@
     fields = groups * comps
     strip_fields = fields + 2 + groups
     nx, ny = lax.axis_size("gx"), lax.axis_size("gy")
-    if depth != 8 or width != 128 or rows_x % 8 or groups != len(SIGMA) or strip_fields % 4:
+    if depth != 8 or width != 128 or rows_x % 8 or groups != len(SIGMA) or strip_fields % 4 or rows_x < 2 * HALO:
         raise ValueError("tile shape")
     if nx % 2:
         raise ValueError("odd axis")
@@ -415,7 +502,6 @@
     rows = rows_x + 2 * HALO
     planes = halo_parts(fields, 2, groups)[2]
     vmem = pl.BlockSpec(memory_space=pltpu.VMEM)
-    smem = pl.BlockSpec(memory_space=pltpu.SMEM)
     hbm = pl.BlockSpec(memory_space=pltpu.HBM)
     small = pltpu.CompilerParams(vmem_limit_bytes=8 * 1024 * 1024)
 
@@ -424,18 +510,18 @@
 
     star_cell = star_cell.reshape(3, 1, slots)
     star_offset = star_offset.reshape(3, 1, slots)
-    arrays = (radiation, ion_fraction, density, star_lum, star_cell, star_offset)
+    arrays = (radiation, ion_fraction, density, star_lum, star_cell, star_offset, star_count)
     sent = strip_fields // 4 * owned + 1
     low_y, high_y, to0, to1, strips, emis = pl.pallas_call(
         pack_kernel,
         out_shape=[
             out(sent), out(sent), out(planes), out(planes), out(strip_fields, tiles), out(groups, rows_x + 1)
         ],
-        in_specs=[hbm] * 6 + [smem],
-        scratch_shapes=[pltpu.VMEM(a.shape, a.dtype) for a in arrays] + [pltpu.SemaphoreType.DMA((6,))],
+        in_specs=[hbm] * 7,
+        scratch_shapes=[pltpu.VMEM(a.shape, a.dtype) for a in arrays] + [pltpu.SemaphoreType.DMA((7,))],
         compiler_params=small,
         name="pack",
-    )(*[pltpu.with_memory_space_constraint(a, pltpu.HBM) for a in arrays], star_count)
+    )(*[pltpu.with_memory_space_constraint(a, pltpu.HBM) for a in arrays[:6]], star_count)
     up = [(i, (i + 1) % ny) for i in range(ny)]
     down = [((i + 1) % ny, i) for i in range(ny)]
     from_low = lax.ppermute(high_y, "gy", up)
@@ -451,25 +537,37 @@
     )(strips, from_low, from_high)
     corner0 = lax.ppermute(edge0, "gx", neighbour_pairs(nx, 0))
     corner1 = lax.ppermute(edge1, "gx", neighbour_pairs(nx, 1))
+    u_mid, ion_mid, saved = pl.pallas_call(
+        inner_kernel,
+        out_shape=[out(fields, rows_x), out(rows_x), out(2, SUBSTEPS, fields)],
+        in_specs=[vmem] * 5,
+        scratch_shapes=[
+            pltpu.VMEM((strip_fields, owned) + plane, f32),
+            pltpu.VMEM((groups, rows_x) + plane, f32),
+            pltpu.VMEM((fields, owned) + plane, f32),
+        ],
+        compiler_params=small,
+        cost_estimate=pl.CostEstimate(flops=40_000_000, bytes_accessed=2_000_000, transcendentals=0),
+        name="inner_rows",
+    )(radiation, ion_fraction, density, joined, emis)
     return tuple(
         pl.pallas_call(
-            step_kernel,
+            outer_kernel,
             out_shape=[
                 jax.ShapeDtypeStruct(radiation.shape, f32),
                 jax.ShapeDtypeStruct(ion_fraction.shape, f32),
             ],
-            in_specs=[vmem] * 9,
+            in_specs=[vmem] * 10,
             scratch_shapes=[
                 pltpu.VMEM((fields, rows) + plane, f32),
-                pltpu.VMEM((rows,) + plane, f32),
                 pltpu.VMEM((rows,) + plane, f32),
                 pltpu.VMEM((strip_fields, tiles) + plane, f32),
                 pltpu.VMEM((groups, rows) + plane, f32),
                 pltpu.VMEM((fields, tiles) + plane, f32),
             ],
             compiler_params=small,
-            name="substeps",
-        )(radiation, ion_fraction, density, from0, from1, joined, corner0, corner1, emis)
+            name="outer_rows",
+        )(u_mid, ion_mid, saved, density, from0, from1, joined, corner0, corner1, emis)
     )
 
 

time: 23.3 us -> 21.4 us (0.918)
  waiting for transfers between devices: 4.8 us -> 1.86 us
  Pallas kernels: 8.58 us -> 9.36 us
    ppermute x1, waiting for transfers between devices: 2.17 us -> 0.01 us  [on_device(): corner1 = lax.ppermute(edge1, 'gx', neighbour_pairs(nx, 1))]
    ppermute x1, waiting for transfers between devices: 0.77 us -> 0.01 us  [on_device(): corner0 = lax.ppermute(edge0, 'gx', neighbour_pairs(nx, 0))]
    pallas_call x1 -> x2, Pallas kernels: 5.12 us -> 5.89 us  [the longest x1 3.11 us: on_device(): pl.pallas_call(outer_kernel, out_shape=[jax.ShapeDtypeStruct(radiation.sh...]
  transfers between devices with their start and end apart: 6 -> 6, of which waited for: 3 -> 1; matrix products, arithmetic and copies ran while one was open for 0% -> 0% of each run, Pallas kernels for 1% -> 14%
where the time goes in v3:
time: 21.4 us; the launch traced here: 21.2 us
  Pallas kernels  9.36 us (44%)
  starting transfers between devices  8.39 us (39%)
  waiting for transfers between devices  1.86 us (9%)
  between operations  1.41 us (7%)
    pallas_call x1, Pallas kernels, on_device(): pl.pallas_call(pack_kernel, out_shape=[out(sent), out(sent), out(planes),...  3.31 us
    ppermute x1, starting transfers between devices, on_device(): from_high = lax.ppermute(low_y, 'gy', down)  3.23 us
    pallas_call x1, Pallas kernels, on_device(): pl.pallas_call(outer_kernel, out_shape=[jax.ShapeDtypeStruct(radiation.sh...  3.11 us
    pallas_call x1, Pallas kernels, on_device(): pl.pallas_call(inner_kernel, out_shape=[out(fields, rows_x), out(rows_x),...  2.78 us
    ppermute x1, starting transfers between devices, on_device(): from1 = lax.ppermute(to1, 'gx', neighbour_pairs(nx, 1))  2.62 us
    ppermute x1, waiting for transfers between devices, on_device(): from_low = lax.ppermute(high_y, 'gy', up)  1.84 us
    ppermute x1, starting transfers between devices, on_device(): from_low = lax.ppermute(high_y, 'gy', up)  1.49 us
    ppermute x1, starting transfers between devices, on_device(): from0 = lax.ppermute(to0, 'gx', neighbour_pairs(nx, 0))  0.56 us
  transfers between devices with their start and end apart: 6, of which 1 were waited for; matrix products, arithmetic and copies ran while one was open for 0% of the time, Pallas kernels for 14%

profile of v3, /device:TPU:0, one launch (start us, length us, event | category | flops | bytes accessed | tf_op | source)
XLA Modules:
  0.0 21.2 jit_solution(10317981296795182722)
XLA Ops:
  0.6 0.0 copy-start
  1.3 3.3 %pack.1 = (f32[7,8,128]{2,1,0:T(8,128)S(1)}, f32[7,8,128]{2,1,0:T(8,128)S(1)}, f32[46,8,128]{2,1,0:T(8,128)S(1)}, f32[46,8,128]{2,1,0:T(8,128)S(1)}, f32[12,3,8,...) custom-call(f32[2,4,8,16,128]{4,3,2,1,0:T(8,128)} %rad.1, f32[8,16,128]{2,1,0:T(8,128)} %ion.1, f32[8,16,128]{2,1,0:T(8,128)} %den.3, ...), custom_call_target="tpu_custom_call" | custom-call | tf_op jit(solution)/shard_map/pack/pallas_call | solution.py:515
  4.7 0.6 %collective-permute-start.2 = (f32[46,8,128]{2,1,0:T(8,128)S(1)}, f32[46,8,128]{2,1,0:T(8,128)S(1)}, u32[]{:S(2)}, u32[]{:S(2)}) collective-permute-start(f32[46,8,128]{2,1,0:T(8,128)S(1)} %get-tuple-element.22), channel_id=1, source_target_pairs={{0,8},{8,0},{16,24},{24,16},{1,9},{9,1},{17,25},{25,17},{2,10},{10... | collective-permute-start | bytes 565256 | tf_op jit(solution)/shard_map/ppermute | solution.py:529
  5.2 2.6 %collective-permute-start.3 = (f32[46,8,128]{2,1,0:T(8,128)S(1)}, f32[46,8,128]{2,1,0:T(8,128)S(1)}, u32[]{:S(2)}, u32[]{:S(2)}) collective-permute-start(f32[46,8,128]{2,1,0:T(8,128)S(1)} %get-tuple-element.23), channel_id=1, source_target_pairs={{0,24},{8,16},{16,8},{24,0},{1,25},{9,17},{17,9},{25,1},{2,26},{10... | collective-permute-start | bytes 565256 | tf_op jit(solution)/shard_map/ppermute | solution.py:530
  7.8 1.5 %collective-permute-start = (f32[7,8,128]{2,1,0:T(8,128)S(1)}, f32[7,8,128]{2,1,0:T(8,128)S(1)}, u32[]{:S(2)}, u32[]{:S(2)}) collective-permute-start(f32[7,8,128]{2,1,0:T(8,128)S(1)} %get-tuple-element.15), channel_id=1, source_target_pairs={{0,1},{1,2},{2,3},{3,4},{4,5},{5,6},{6,7},{7,0},{8,9},{9,10},{10,1... | collective-permute-start | bytes 86024 | tf_op jit(solution)/shard_map/ppermute | solution.py:527
  9.3 3.2 %collective-permute-start.1 = (f32[7,8,128]{2,1,0:T(8,128)S(1)}, f32[7,8,128]{2,1,0:T(8,128)S(1)}, u32[]{:S(2)}, u32[]{:S(2)}) collective-permute-start(f32[7,8,128]{2,1,0:T(8,128)S(1)} %get-tuple-element.16), channel_id=1, source_target_pairs={{1,0},{2,1},{3,2},{4,3},{5,4},{6,5},{7,6},{0,7},{9,8},{10,9},{11,1... | collective-permute-start | bytes 86024 | tf_op jit(solution)/shard_map/ppermute | solution.py:528
  12.6 1.8 %collective-permute-done.from_low = f32[7,8,128]{2,1,0:T(8,128)S(1)} collective-permute-done((f32[7,8,128]{2,1,0:T(8,128)S(1)}, f32[7,8,128]{2,1,0:T(8,128)S(1)}, u32[]{:S(2)}, u32[]{:S(2)}) %collective-permute-start) | collective-permute-done | bytes 28704 | tf_op jit(solution)/shard_map/ppermute | solution.py:527
  14.4 0.0 collective-permute-done.1.from_high
  14.4 0.0 copy-start.1
  14.4 0.0 copy-start.2
  14.4 0.2 edges.1
  14.6 0.1 collective-permute-start.4
  14.7 0.4 %collective-permute-start.5 = (f32[7,8,128]{2,1,0:T(8,128)S(1)}, f32[7,8,128]{2,1,0:T(8,128)S(1)}, u32[]{:S(2)}, u32[]{:S(2)}) collective-permute-start(f32[7,8,128]{2,1,0:T(8,128)S(1)} %get-tuple-element.25), channel_id=1, source_target_pairs={{0,24},{8,16},{16,8},{24,0},{1,25},{9,17},{17,9},{25,1},{2,26},{10... | collective-permute-start | bytes 86024 | tf_op jit(solution)/shard_map/ppermute | solution.py:539
  15.1 0.0 copy-done
  15.1 0.2 copy-done.1
  15.3 0.0 copy-done.2
  15.3 2.8 %inner_rows.1 = (f32[8,16,8,128]{3,2,1,0:T(8,128)S(1)}, f32[16,8,128]{2,1,0:T(8,128)S(1)}, f32[2,4,8,8,128]{4,3,2,1,0:T(8,128)S(1)}) custom-call(f32[2,4,8,16,128]{4,3,2,1,0:T(8,128)S(1)} %copy-done, f32[8,16,128]{2,1,0:T(8,128)S(1)} %copy-done.2, f32[8,16,128]{2,1,0:T(8,128)S(1)} %copy-done.1, f32[12,3,8,128]{3,2,1,0:T(8,128)S(1)} %get-tuple-element.17.joined, ...), custom_call_target="tpu_custom_call" | custom-call | flops 40000000 | bytes 2000000 | tf_op jit(solution)/shard_map/inner_rows/pallas_call | solution.py:540
  18.1 0.0 collective-permute-done.4.corner0
  18.1 0.0 collective-permute-done.5.corner1
  18.1 0.0 collective-permute-done.2.from0
  18.1 0.0 collective-permute-done.3.from1
  18.1 3.1 %outer_rows.1 = (f32[2,4,8,16,128]{4,3,2,1,0:T(8,128)}, f32[8,16,128]{2,1,0:T(8,128)}) custom-call(f32[8,16,8,128]{3,2,1,0:T(8,128)S(1)} %get-tuple-element.19.u_mid, f32[16,8,128]{2,1,0:T(8,128)S(1)} %get-tuple-element.20.ion_mid, f32[2,4,8,8,128]{4,3,2,1,0:T(8,128)S(1)} %get-tuple-element.21.saved, f32[8,16,128]{2,1,0:T(8,128)S(1)} %copy-done.1, ...), custom_call_target="tpu_custom_call" | custom-call | tf_op jit(solution)/shard_map/outer_rows/pallas_call | solution.py:554
Async XLA Ops:
  0.6 14.5 %copy-start = (f32[2,4,8,16,128]{4,3,2,1,0:T(8,128)S(1)}, f32[2,4,8,16,128]{4,3,2,1,0:T(8,128)}, u32[]{:S(2)}) copy-start(f32[2,4,8,16,128]{4,3,2,1,0:T(8,128)} %rad.1) | copy-start | bytes 1572868
  4.7 13.4 %collective-permute-start.2 = (f32[46,8,128]{2,1,0:T(8,128)S(1)}, f32[46,8,128]{2,1,0:T(8,128)S(1)}, u32[]{:S(2)}, u32[]{:S(2)}) collective-permute-start(f32[46,8,128]{2,1,0:T(8,128)S(1)} %get-tuple-element.22), channel_id=1, source_target_pairs={{0,8},{8,0},{16,24},{24,16},{1,9},{9,1},{17,25},{25,17},{2,10},{10... | collective-permute-start | bytes 565256 | tf_op jit(solution)/shard_map/ppermute | solution.py:529
  5.2 12.9 %collective-permute-start.3 = (f32[46,8,128]{2,1,0:T(8,128)S(1)}, f32[46,8,128]{2,1,0:T(8,128)S(1)}, u32[]{:S(2)}, u32[]{:S(2)}) collective-permute-start(f32[46,8,128]{2,1,0:T(8,128)S(1)} %get-tuple-element.23), channel_id=1, source_target_pairs={{0,24},{8,16},{16,8},{24,0},{1,25},{9,17},{17,9},{25,1},{2,26},{10... | collective-permute-start | bytes 565256 | tf_op jit(solution)/shard_map/ppermute | solution.py:530
  7.8 6.6 %collective-permute-start = (f32[7,8,128]{2,1,0:T(8,128)S(1)}, f32[7,8,128]{2,1,0:T(8,128)S(1)}, u32[]{:S(2)}, u32[]{:S(2)}) collective-permute-start(f32[7,8,128]{2,1,0:T(8,128)S(1)} %get-tuple-element.15), channel_id=1, source_target_pairs={{0,1},{1,2},{2,3},{3,4},{4,5},{5,6},{6,7},{7,0},{8,9},{9,10},{10,1... | collective-permute-start | bytes 86024 | tf_op jit(solution)/shard_map/ppermute | solution.py:527
  9.3 5.1 %collective-permute-start.1 = (f32[7,8,128]{2,1,0:T(8,128)S(1)}, f32[7,8,128]{2,1,0:T(8,128)S(1)}, u32[]{:S(2)}, u32[]{:S(2)}) collective-permute-start(f32[7,8,128]{2,1,0:T(8,128)S(1)} %get-tuple-element.16), channel_id=1, source_target_pairs={{1,0},{2,1},{3,2},{4,3},{5,4},{6,5},{7,6},{0,7},{9,8},{10,9},{11,1... | collective-permute-start | bytes 86024 | tf_op jit(solution)/shard_map/ppermute | solution.py:528
  14.4 0.8 %copy-start.1 = (f32[8,16,128]{2,1,0:T(8,128)S(1)}, f32[8,16,128]{2,1,0:T(8,128)}, u32[]{:S(2)}) copy-start(f32[8,16,128]{2,1,0:T(8,128)} %den.3) | copy-start | bytes 196612
  14.4 0.9 %copy-start.2 = (f32[8,16,128]{2,1,0:T(8,128)S(1)}, f32[8,16,128]{2,1,0:T(8,128)}, u32[]{:S(2)}) copy-start(f32[8,16,128]{2,1,0:T(8,128)} %ion.1) | copy-start | bytes 196612
  14.6 3.5 %collective-permute-start.4 = (f32[7,8,128]{2,1,0:T(8,128)S(1)}, f32[7,8,128]{2,1,0:T(8,128)S(1)}, u32[]{:S(2)}, u32[]{:S(2)}) collective-permute-start(f32[7,8,128]{2,1,0:T(8,128)S(1)} %get-tuple-element.24), channel_id=1, source_target_pairs={{0,8},{8,0},{16,24},{24,16},{1,9},{9,1},{17,25},{25,17},{2,10},{10... | collective-permute-start | bytes 86024 | tf_op jit(solution)/shard_map/ppermute | solution.py:538
  14.7 3.4 %collective-permute-start.5 = (f32[7,8,128]{2,1,0:T(8,128)S(1)}, f32[7,8,128]{2,1,0:T(8,128)S(1)}, u32[]{:S(2)}, u32[]{:S(2)}) collective-permute-start(f32[7,8,128]{2,1,0:T(8,128)S(1)} %get-tuple-element.25), channel_id=1, source_target_pairs={{0,24},{8,16},{16,8},{24,0},{1,25},{9,17},{17,9},{25,1},{2,26},{10... | collective-permute-start | bytes 86024 | tf_op jit(solution)/shard_map/ppermute | solution.py:539

commit v4 on v3

--- a/solution.py
+++ b/solution.py
@@ -46,6 +46,11 @@
         precision=lax.Precision.HIGHEST,
         preferred_element_type=jnp.float32,
     )
+
+
+def sizes_of(emis, fields):
+    groups, rows, depth, width = emis.shape
+    return groups, fields // groups, depth, rows - 1, width
 
 
 def strip_lane():
@@ -74,7 +79,7 @@
     ]
     for copy in copies:
         copy.start()
-    groups, comps, depth, rows_x, width = rad.shape
+    groups, comps, depth, rows_x, width = sizes_of(emis, rad.shape[0])
     owned = rows_x // 8
     lane = strip_lane()
     column = lax.rem(lane, 16)
@@ -97,8 +102,8 @@
 
     for copy in copies[4:]:
         copy.wait()
-    reads = [(lambda x, g=g, c=c: rad[g, c, :, x, :]) for g in range(groups) for c in range(comps)]
-    reads += [lambda x: ion[:, x, :], lambda x: den[:, x, :]]
+    reads = [(lambda x, f=f: rad[f, pl.ds(x, depth, stride=rows_x), :]) for f in range(groups * comps)]
+    reads += [lambda x: ion[pl.ds(x, depth, stride=rows_x), :], lambda x: den[pl.ds(x, depth, stride=rows_x), :]]
     fields = len(reads)
     packs_low = [[zero] * owned for _ in range((fields + groups) // 4)]
     packs_high = [[zero] * owned for _ in range((fields + groups) // 4)]
@@ -111,11 +116,10 @@
         for v in range(owned):
             acc = zero
             for group in range(8):
-                plane = read(8 * v + group)
-                low = pltpu.roll(plane, (16 * group + 4) % 128, 1)
-                high = pltpu.roll(plane, (16 * group + 12) % 128, 1)
+                low = pltpu.roll(read(8 * v + group), (16 * group + 4) % 128, 1)
                 at = lane - 16 * group
-                acc = jnp.where((at >= 0) & (at < 8), low, jnp.where((at >= 8) & (at < 16), high, acc))
+                acc = jnp.where((at >= 0) & (at < 8), low, acc)
+            acc = jnp.where(column < 8, acc, pltpu.roll(acc, 8, 1))
             strips[f, v] = acc
             p, k = f // 4, f % 4
             packs_high[p][v] = add(packs_high[p][v], k, acc, 8)
@@ -123,22 +127,25 @@
     for g in range(groups):
         f = fields + g
         p, k = f // 4, f % 4
-        sent, own = [zero] * (owned + 1), [zero] * (owned + 1)
+        near, past = [zero] * (owned + 1), [zero] * (owned + 1)
         for x in range(rows_x + 1):
             v, group = x // 8, x % 8
-            plane, past = plane_of(g, x, 0), plane_of(g, x, 1)
+            plane = plane_of(g, x, 0)
             emis[g, x] = plane
+            at = lane - 16 * group
             low = pltpu.roll(plane, (16 * group + 4) % 128, 1)
-            high = pltpu.roll(plane, (16 * group + 12) % 128, 1)
-            past_low = pltpu.roll(past, (16 * group + 4) % 128, 1)
-            past_high = pltpu.roll(past, (16 * group + 12) % 128, 1)
-            at = lane - 16 * group
-            s = jnp.where((at >= 4) & (at < 8), low, sent[v])
-            s = jnp.where((at >= 8) & (at < 12), high, s)
-            sent[v] = jnp.where(at == 12, past_high, s)
-            o = jnp.where((at >= 0) & (at < 4), low, own[v])
-            o = jnp.where((at >= 12) & (at < 16), high, o)
-            own[v] = jnp.where(at == 4, past_low, o)
+            near[v] = jnp.where((at >= 0) & (at < 8), low, near[v])
+            over = plane_of(g, x, 1)
+            over = pltpu.roll(over, 16 * group, 1) if group else over
+            past[v] = jnp.where(at == 0, over, past[v])
+        sent, own = [], []
+        for v in range(owned + 1):
+            far = pltpu.roll(near[v], 8, 1)
+            s = jnp.where((column >= 4) & (column < 8), near[v], 0.0)
+            s = jnp.where((column >= 8) & (column < 12), far, s)
+            sent.append(jnp.where(column == 12, pltpu.roll(past[v], 12, 1), s))
+            o = jnp.where(column < 4, near[v], jnp.where(column >= 12, far, 0.0))
+            own.append(jnp.where(column == 4, pltpu.roll(past[v], 4, 1), o))
         for v in range(owned + 1):
             strips[f, v] = own[v]
         for v in range(owned):
@@ -161,13 +168,12 @@
         to1[at] = jnp.where(even, low, high)
         at += 1
 
-    for g in range(groups):
-        for c in range(comps):
-            for i in range(HALO):
-                put(rad[g, c, :, rows_x - HALO + i, :], rad[g, c, :, i, :])
-    for ref in (ion, den):
+    for read in reads[: groups * comps]:
+        for i in range(HALO):
+            put(read(rows_x - HALO + i), read(i))
+    for read in reads[groups * comps :]:
         for i in range(INNER):
-            put(ref[:, rows_x - INNER + i, :], ref[:, i, :])
+            put(read(rows_x - INNER + i), read(i))
     for g in range(groups):
         for i in range(INNER + 1):
             put(plane_of(g, rows_x - INNER + i, 0), plane_of(g, i, 0))
@@ -332,16 +338,16 @@
 
 
 def inner_kernel(rad, ion, den, joined, emis, u_ref, ion_ref, saved, s_ref, e_ref, t_ref):
-    groups, comps, depth, rows_x, width = rad.shape
+    groups, comps, depth, rows_x, width = sizes_of(emis, rad.shape[0])
     tiles = rows_x // 8
     fields = groups * comps
     lane = strip_lane()
     for g in range(groups):
         for c in range(comps):
             for x in range(rows_x):
-                u_ref[g * comps + c, x] = rad[g, c, :, x, :]
+                u_ref[g * comps + c, x] = rad[g * comps + c, pl.ds(x, depth, stride=rows_x), :]
     for x in range(rows_x):
-        ion_ref[x] = ion[:, x, :]
+        ion_ref[x] = ion[pl.ds(x, depth, stride=rows_x), :]
     for f in range(fields + 2):
         for v in range(tiles):
             s_ref[f, v] = joined[f, v]
@@ -367,7 +373,7 @@
             lambda k, x: u_ref[k, x],
             lambda g, x: e_ref[g, x],
             lambda x: ion_ref[x],
-            lambda x: den[:, x, :],
+            lambda x: den[pl.ds(x, depth, stride=rows_x), :],
             write,
             t_ref,
             groups,
@@ -383,7 +389,7 @@
     rad_out, ion_out, u_ref, ion_ref, s_ref, e_ref, t_ref,
 ):
     even = lax.rem(lax.axis_index("gx"), 2) == 0
-    groups, comps, depth, rows_x, width = rad_out.shape
+    groups, comps, depth, rows_x, width = sizes_of(emis, rad_out.shape[0])
     tiles = joined.shape[1]
     owned = tiles - 1
     cycle = 8 * tiles
@@ -447,12 +453,12 @@
             return beside(inner_at + INNER + x + INNER)[0]
         if x >= rows_x:
             return beside(inner_at + INNER + x - rows_x)[1]
-        return den[:, x, :]
+        return den[pl.ds(x, depth, stride=rows_x), :]
 
     def finish(x, values, frac):
         for k, value in enumerate(values):
-            rad_out[k // comps, k % comps, :, x, :] = value
-        ion_out[:, x, :] = frac
+            rad_out[k, pl.ds(x, depth, stride=rows_x), :] = value
+        ion_out[pl.ds(x, depth, stride=rows_x), :] = frac
 
     def write(x, values, frac):
         for k, value in enumerate(values):
@@ -508,6 +514,10 @@
     def out(*shape):
         return jax.ShapeDtypeStruct(shape + plane, f32)
 
+    shapes = radiation.shape, ion_fraction.shape
+    radiation = radiation.reshape(fields, depth * rows_x, width)
+    ion_fraction = ion_fraction.reshape(depth * rows_x, width)
+    density = density.reshape(depth * rows_x, width)
     star_cell = star_cell.reshape(3, 1, slots)
     star_offset = star_offset.reshape(3, 1, slots)
     arrays = (radiation, ion_fraction, density, star_lum, star_cell, star_offset, star_count)
@@ -551,7 +561,8 @@
         name="inner_rows",
     )(radiation, ion_fraction, density, joined, emis)
     return tuple(
-        pl.pallas_call(
+        result.reshape(shape)
+        for shape, result in zip(shapes, pl.pallas_call(
             outer_kernel,
             out_shape=[
                 jax.ShapeDtypeStruct(radiation.shape, f32),
@@ -567,7 +578,7 @@
             ],
             compiler_params=small,
             name="outer_rows",
-        )(u_mid, ion_mid, saved, density, from0, from1, joined, corner0, corner1, emis)
+        )(u_mid, ion_mid, saved, density, from0, from1, joined, corner0, corner1, emis))
     )
 
 

time: 21.4 us -> 20.8 us (0.972)
  Pallas kernels: 9.36 us -> 8.39 us
  waiting for transfers between devices: 1.86 us -> 2.22 us
    pallas_call x1, Pallas kernels: 2.78 us -> 2.35 us  [on_device(): pl.pallas_call(inner_kernel, out_shape=[out(fields, rows_x), out(rows_x),...]
    ppermute x1, waiting for transfers between devices: 0.01 us -> 0.37 us  [on_device(): corner1 = lax.ppermute(edge1, 'gx', neighbour_pairs(nx, 1))]
    pallas_call x1, Pallas kernels: 3.31 us -> 3.01 us  [on_device(): pl.pallas_call(pack_kernel, out_shape=[out(sent), out(sent), out(planes),...]
    pallas_call x1, Pallas kernels: 3.11 us -> 2.86 us  [on_device(): pl.pallas_call(outer_kernel, out_shape=[jax.ShapeDtypeStruct(radiation.sh...]
  transfers between devices with their start and end apart: 6 -> 6, of which waited for: 1 -> 2; matrix products, arithmetic and copies ran while one was open for 0% -> 0% of each run, Pallas kernels for 14% -> 12%
where the time goes in v4:
time: 20.8 us; the launch traced here: 20.6 us
  Pallas kernels  8.39 us (40%)
  starting transfers between devices  8.39 us (40%)
  waiting for transfers between devices  2.22 us (11%)
  between operations  1.39 us (7%)
  local copies, waits for them, and re-layouts  0.21 us (1%)
    ppermute x1, starting transfers between devices, on_device(): from_high = lax.ppermute(low_y, 'gy', down)  3.23 us
    pallas_call x1, Pallas kernels, on_device(): pl.pallas_call(pack_kernel, out_shape=[out(sent), out(sent), out(planes),...  3.01 us
    pallas_call x1, Pallas kernels, on_device(): pl.pallas_call(outer_kernel, out_shape=[jax.ShapeDtypeStruct(radiation.sh...  2.86 us
    ppermute x1, starting transfers between devices, on_device(): from1 = lax.ppermute(to1, 'gx', neighbour_pairs(nx, 1))  2.62 us
    pallas_call x1, Pallas kernels, on_device(): pl.pallas_call(inner_kernel, out_shape=[out(fields, rows_x), out(rows_x),...  2.35 us
    ppermute x1, waiting for transfers between devices, on_device(): from_low = lax.ppermute(high_y, 'gy', up)  1.84 us
    ppermute x1, starting transfers between devices, on_device(): from_low = lax.ppermute(high_y, 'gy', up)  1.49 us
    ppermute x1, starting transfers between devices, on_device(): from0 = lax.ppermute(to0, 'gx', neighbour_pairs(nx, 0))  0.56 us
  transfers between devices with their start and end apart: 6, of which 2 were waited for; matrix products, arithmetic and copies ran while one was open for 0% of the time, Pallas kernels for 12%

profile of v4, /device:TPU:0, one launch (start us, length us, event | category | flops | bytes accessed | tf_op | source)
XLA Modules:
  0.0 20.6 jit_solution(13683706237938838474)
XLA Ops:
  0.6 0.0 copy-start
  1.3 3.0 %pack.1 = (f32[7,8,128]{2,1,0:T(8,128)S(1)}, f32[7,8,128]{2,1,0:T(8,128)S(1)}, f32[46,8,128]{2,1,0:T(8,128)S(1)}, f32[46,8,128]{2,1,0:T(8,128)S(1)}, f32[12,3,8,...) custom-call(f32[8,128,128]{2,1,0:T(8,128)} %bitcast.7, f32[128,128]{1,0:T(8,128)} %bitcast.12, f32[128,128]{1,0:T(8,128)} %bitcast.9, ...), custom_call_target="tpu_custom_call" | custom-call | tf_op jit(solution)/shard_map/pack/pallas_call | solution.py:525
  4.4 0.6 %collective-permute-start.2 = (f32[46,8,128]{2,1,0:T(8,128)S(1)}, f32[46,8,128]{2,1,0:T(8,128)S(1)}, u32[]{:S(2)}, u32[]{:S(2)}) collective-permute-start(f32[46,8,128]{2,1,0:T(8,128)S(1)} %get-tuple-element.24), channel_id=1, source_target_pairs={{0,8},{8,0},{16,24},{24,16},{1,9},{9,1},{17,25},{25,17},{2,10},{10... | collective-permute-start | bytes 565256 | tf_op jit(solution)/shard_map/ppermute | solution.py:539
  4.9 2.6 %collective-permute-start.3 = (f32[46,8,128]{2,1,0:T(8,128)S(1)}, f32[46,8,128]{2,1,0:T(8,128)S(1)}, u32[]{:S(2)}, u32[]{:S(2)}) collective-permute-start(f32[46,8,128]{2,1,0:T(8,128)S(1)} %get-tuple-element.25), channel_id=1, source_target_pairs={{0,24},{8,16},{16,8},{24,0},{1,25},{9,17},{17,9},{25,1},{2,26},{10... | collective-permute-start | bytes 565256 | tf_op jit(solution)/shard_map/ppermute | solution.py:540
  7.5 1.5 %collective-permute-start = (f32[7,8,128]{2,1,0:T(8,128)S(1)}, f32[7,8,128]{2,1,0:T(8,128)S(1)}, u32[]{:S(2)}, u32[]{:S(2)}) collective-permute-start(f32[7,8,128]{2,1,0:T(8,128)S(1)} %get-tuple-element.17), channel_id=1, source_target_pairs={{0,1},{1,2},{2,3},{3,4},{4,5},{5,6},{6,7},{7,0},{8,9},{9,10},{10,1... | collective-permute-start | bytes 86024 | tf_op jit(solution)/shard_map/ppermute | solution.py:537
  9.0 3.2 %collective-permute-start.1 = (f32[7,8,128]{2,1,0:T(8,128)S(1)}, f32[7,8,128]{2,1,0:T(8,128)S(1)}, u32[]{:S(2)}, u32[]{:S(2)}) collective-permute-start(f32[7,8,128]{2,1,0:T(8,128)S(1)} %get-tuple-element.18), channel_id=1, source_target_pairs={{1,0},{2,1},{3,2},{4,3},{5,4},{6,5},{7,6},{0,7},{9,8},{10,9},{11,1... | collective-permute-start | bytes 86024 | tf_op jit(solution)/shard_map/ppermute | solution.py:538
  12.3 1.8 %collective-permute-done.from_low = f32[7,8,128]{2,1,0:T(8,128)S(1)} collective-permute-done((f32[7,8,128]{2,1,0:T(8,128)S(1)}, f32[7,8,128]{2,1,0:T(8,128)S(1)}, u32[]{:S(2)}, u32[]{:S(2)}) %collective-permute-start) | collective-permute-done | bytes 28704 | tf_op jit(solution)/shard_map/ppermute | solution.py:537
  14.1 0.0 collective-permute-done.1.from_high
  14.1 0.0 copy-start.1
  14.1 0.0 copy-start.2
  14.1 0.2 edges.1
  14.3 0.1 collective-permute-start.4
  14.4 0.4 %collective-permute-start.5 = (f32[7,8,128]{2,1,0:T(8,128)S(1)}, f32[7,8,128]{2,1,0:T(8,128)S(1)}, u32[]{:S(2)}, u32[]{:S(2)}) collective-permute-start(f32[7,8,128]{2,1,0:T(8,128)S(1)} %get-tuple-element.27), channel_id=1, source_target_pairs={{0,24},{8,16},{16,8},{24,0},{1,25},{9,17},{17,9},{25,1},{2,26},{10... | collective-permute-start | bytes 86024 | tf_op jit(solution)/shard_map/ppermute | solution.py:549
  14.8 0.0 copy-done
  14.8 0.2 copy-done.1
  15.0 0.0 copy-done.2
  15.0 2.4 %inner_rows.1 = (f32[8,16,8,128]{3,2,1,0:T(8,128)S(1)}, f32[16,8,128]{2,1,0:T(8,128)S(1)}, f32[2,4,8,8,128]{4,3,2,1,0:T(8,128)S(1)}) custom-call(f32[8,128,128]{2,1,0:T(8,128)S(1)} %bitcast.8, f32[128,128]{1,0:T(8,128)S(1)} %bitcast.13, f32[128,128]{1,0:T(8,128)S(1)} %bitcast.10, f32[12,3,8,128]{3,2,1,0:T(8,128)S(1)} %get-tuple-element.19.joined, ...), custom_call_target="tpu_custom_call" | custom-call | flops 40000000 | bytes 2000000 | tf_op jit(solution)/shard_map/inner_rows/pallas_call | solution.py:550
  17.3 0.0 collective-permute-done.4.corner0
  17.4 0.4 %collective-permute-done.5.corner1 = f32[7,8,128]{2,1,0:T(8,128)S(1)} collective-permute-done((f32[7,8,128]{2,1,0:T(8,128)S(1)}, f32[7,8,128]{2,1,0:T(8,128)S(1)}, u32[]{:S(2)}, u32[]{:S(2)}) %collective-permute-start.5) | collective-permute-done | bytes 28704 | tf_op jit(solution)/shard_map/ppermute | solution.py:549
  17.7 0.0 collective-permute-done.2.from0
  17.7 0.0 collective-permute-done.3.from1
  17.7 2.9 %outer_rows.1 = (f32[8,128,128]{2,1,0:T(8,128)}, f32[128,128]{1,0:T(8,128)}) custom-call(f32[8,16,8,128]{3,2,1,0:T(8,128)S(1)} %get-tuple-element.21.u_mid, f32[16,8,128]{2,1,0:T(8,128)S(1)} %get-tuple-element.22.ion_mid, f32[2,4,8,8,128]{4,3,2,1,0:T(8,128)S(1)} %get-tuple-element.23.saved, f32[128,128]{1,0:T(8,128)S(1)} %bitcast.11, ...), custom_call_target="tpu_custom_call" | custom-call | tf_op jit(solution)/shard_map/outer_rows/pallas_call | solution.py:565
Async XLA Ops:
  0.6 14.2 %copy-start = (f32[2,4,8,16,128]{4,3,2,1,0:T(8,128)S(1)}, f32[2,4,8,16,128]{4,3,2,1,0:T(8,128)}, u32[]{:S(2)}) copy-start(f32[2,4,8,16,128]{4,3,2,1,0:T(8,128)} %param.7) | copy-start | bytes 1572868
  4.4 13.4 %collective-permute-start.2 = (f32[46,8,128]{2,1,0:T(8,128)S(1)}, f32[46,8,128]{2,1,0:T(8,128)S(1)}, u32[]{:S(2)}, u32[]{:S(2)}) collective-permute-start(f32[46,8,128]{2,1,0:T(8,128)S(1)} %get-tuple-element.24), channel_id=1, source_target_pairs={{0,8},{8,0},{16,24},{24,16},{1,9},{9,1},{17,25},{25,17},{2,10},{10... | collective-permute-start | bytes 565256 | tf_op jit(solution)/shard_map/ppermute | solution.py:539
  4.9 12.8 %collective-permute-start.3 = (f32[46,8,128]{2,1,0:T(8,128)S(1)}, f32[46,8,128]{2,1,0:T(8,128)S(1)}, u32[]{:S(2)}, u32[]{:S(2)}) collective-permute-start(f32[46,8,128]{2,1,0:T(8,128)S(1)} %get-tuple-element.25), channel_id=1, source_target_pairs={{0,24},{8,16},{16,8},{24,0},{1,25},{9,17},{17,9},{25,1},{2,26},{10... | collective-permute-start | bytes 565256 | tf_op jit(solution)/shard_map/ppermute | solution.py:540
  7.5 6.6 %collective-permute-start = (f32[7,8,128]{2,1,0:T(8,128)S(1)}, f32[7,8,128]{2,1,0:T(8,128)S(1)}, u32[]{:S(2)}, u32[]{:S(2)}) collective-permute-start(f32[7,8,128]{2,1,0:T(8,128)S(1)} %get-tuple-element.17), channel_id=1, source_target_pairs={{0,1},{1,2},{2,3},{3,4},{4,5},{5,6},{6,7},{7,0},{8,9},{9,10},{10,1... | collective-permute-start | bytes 86024 | tf_op jit(solution)/shard_map/ppermute | solution.py:537
  9.0 5.1 %collective-permute-start.1 = (f32[7,8,128]{2,1,0:T(8,128)S(1)}, f32[7,8,128]{2,1,0:T(8,128)S(1)}, u32[]{:S(2)}, u32[]{:S(2)}) collective-permute-start(f32[7,8,128]{2,1,0:T(8,128)S(1)} %get-tuple-element.18), channel_id=1, source_target_pairs={{1,0},{2,1},{3,2},{4,3},{5,4},{6,5},{7,6},{0,7},{9,8},{10,9},{11,1... | collective-permute-start | bytes 86024 | tf_op jit(solution)/shard_map/ppermute | solution.py:538
  14.1 0.8 %copy-start.1 = (f32[8,16,128]{2,1,0:T(8,128)S(1)}, f32[8,16,128]{2,1,0:T(8,128)}, u32[]{:S(2)}) copy-start(f32[8,16,128]{2,1,0:T(8,128)} %param.9) | copy-start | bytes 196612
  14.1 0.9 %copy-start.2 = (f32[8,16,128]{2,1,0:T(8,128)S(1)}, f32[8,16,128]{2,1,0:T(8,128)}, u32[]{:S(2)}) copy-start(f32[8,16,128]{2,1,0:T(8,128)} %param.8) | copy-start | bytes 196612
  14.3 3.1 %collective-permute-start.4 = (f32[7,8,128]{2,1,0:T(8,128)S(1)}, f32[7,8,128]{2,1,0:T(8,128)S(1)}, u32[]{:S(2)}, u32[]{:S(2)}) collective-permute-start(f32[7,8,128]{2,1,0:T(8,128)S(1)} %get-tuple-element.26), channel_id=1, source_target_pairs={{0,8},{8,0},{16,24},{24,16},{1,9},{9,1},{17,25},{25,17},{2,10},{10... | collective-permute-start | bytes 86024 | tf_op jit(solution)/shard_map/ppermute | solution.py:548
  14.4 3.4 %collective-permute-start.5 = (f32[7,8,128]{2,1,0:T(8,128)S(1)}, f32[7,8,128]{2,1,0:T(8,128)S(1)}, u32[]{:S(2)}, u32[]{:S(2)}) collective-permute-start(f32[7,8,128]{2,1,0:T(8,128)S(1)} %get-tuple-element.27), channel_id=1, source_target_pairs={{0,24},{8,16},{16,8},{24,0},{1,25},{9,17},{17,9},{25,1},{2,26},{10... | collective-permute-start | bytes 86024 | tf_op jit(solution)/shard_map/ppermute | solution.py:549

commit v5 on v4

--- a/solution.py
+++ b/solution.py
@@ -4,6 +4,7 @@
 from jax.experimental import pallas as pl
 from jax.experimental.pallas import tpu as pltpu
 from jax.sharding import PartitionSpec as P
+
 
 SUBSTEPS = 4
 CHEM_ITERS = 3
@@ -181,7 +182,7 @@
 
 def edge_kernel(strips, from_low, from_high, joined, to0, to1):
     even = lax.rem(lax.axis_index("gx"), 2) == 0
-    fields, tiles, depth, width = strips.shape
+    fields, tiles, _, width = strips.shape
     owned = tiles - 1
     groups = len(SIGMA)
     lane = strip_lane()
@@ -240,7 +241,7 @@
     loss = ALPHA * reach
     push = [state[g][0] * (DT * SIGMA[g]) for g in range(groups)]
     frac = ion
-    for step in range(CHEM_ITERS):
+    for _ in range(CHEM_ITERS):
         free = reach * (1.0 - frac)
         atten = [1.0 / (1.0 + SIGMA[g] * free) for g in range(groups)]
         gamma = sum((push[g] * atten[g] for g in range(1, groups)), push[0] * atten[0])
@@ -338,7 +339,7 @@
 
 
 def inner_kernel(rad, ion, den, joined, emis, u_ref, ion_ref, saved, s_ref, e_ref, t_ref):
-    groups, comps, depth, rows_x, width = sizes_of(emis, rad.shape[0])
+    groups, comps, depth, rows_x, _ = sizes_of(emis, rad.shape[0])
     tiles = rows_x // 8
     fields = groups * comps
     lane = strip_lane()
@@ -534,10 +535,10 @@
     )(*[pltpu.with_memory_space_constraint(a, pltpu.HBM) for a in arrays[:6]], star_count)
     up = [(i, (i + 1) % ny) for i in range(ny)]
     down = [((i + 1) % ny, i) for i in range(ny)]
+    from1 = lax.ppermute(to1, "gx", neighbour_pairs(nx, 1))
     from_low = lax.ppermute(high_y, "gy", up)
     from_high = lax.ppermute(low_y, "gy", down)
     from0 = lax.ppermute(to0, "gx", neighbour_pairs(nx, 0))
-    from1 = lax.ppermute(to1, "gx", neighbour_pairs(nx, 1))
     joined, edge0, edge1 = pl.pallas_call(
         edge_kernel,
         out_shape=[out(strip_fields, tiles), out(strip_fields // 2 + 1), out(strip_fields // 2 + 1)],

time: 20.8 us -> 20.8 us (level)
  no operation moved by 1% of the time
where the time goes in v5:
time: 20.8 us; the launch traced here: 20.6 us
  Pallas kernels  8.39 us (40%)
  starting transfers between devices  8.39 us (40%)
  waiting for transfers between devices  2.22 us (11%)
  between operations  1.39 us (7%)
  local copies, waits for them, and re-layouts  0.21 us (1%)
    ppermute x1, starting transfers between devices, on_device(): from_high = lax.ppermute(low_y, 'gy', down)  3.23 us
    pallas_call x1, Pallas kernels, on_device(): pl.pallas_call(pack_kernel, out_shape=[out(sent), out(sent), out(planes),...  3.01 us
    pallas_call x1, Pallas kernels, on_device(): pl.pallas_call(outer_kernel, out_shape=[jax.ShapeDtypeStruct(radiation.sh...  2.86 us
    ppermute x1, starting transfers between devices, on_device(): from1 = lax.ppermute(to1, 'gx', neighbour_pairs(nx, 1))  2.62 us
    pallas_call x1, Pallas kernels, on_device(): pl.pallas_call(inner_kernel, out_shape=[out(fields, rows_x), out(rows_x),...  2.35 us
    ppermute x1, waiting for transfers between devices, on_device(): from_low = lax.ppermute(high_y, 'gy', up)  1.84 us
    ppermute x1, starting transfers between devices, on_device(): from_low = lax.ppermute(high_y, 'gy', up)  1.49 us
    ppermute x1, starting transfers between devices, on_device(): from0 = lax.ppermute(to0, 'gx', neighbour_pairs(nx, 0))  0.56 us
  transfers between devices with their start and end apart: 6, of which 2 were waited for; matrix products, arithmetic and copies ran while one was open for 0% of the time, Pallas kernels for 12%

profile of v5, /device:TPU:0, one launch (start us, length us, event | category | flops | bytes accessed | tf_op | source)
XLA Modules:
  0.0 20.6 jit_solution(13683706237938838474)
XLA Ops:
  0.6 0.0 copy-start
  1.3 3.0 %pack.1 = (f32[7,8,128]{2,1,0:T(8,128)S(1)}, f32[7,8,128]{2,1,0:T(8,128)S(1)}, f32[46,8,128]{2,1,0:T(8,128)S(1)}, f32[46,8,128]{2,1,0:T(8,128)S(1)}, f32[12,3,8,...) custom-call(f32[8,128,128]{2,1,0:T(8,128)} %bitcast.7, f32[128,128]{1,0:T(8,128)} %bitcast.12, f32[128,128]{1,0:T(8,128)} %bitcast.9, ...), custom_call_target="tpu_custom_call" | custom-call | tf_op jit(solution)/shard_map/pack/pallas_call | solution.py:526
  4.4 0.6 %collective-permute-start.2 = (f32[46,8,128]{2,1,0:T(8,128)S(1)}, f32[46,8,128]{2,1,0:T(8,128)S(1)}, u32[]{:S(2)}, u32[]{:S(2)}) collective-permute-start(f32[46,8,128]{2,1,0:T(8,128)S(1)} %get-tuple-element.24), channel_id=1, source_target_pairs={{0,8},{8,0},{16,24},{24,16},{1,9},{9,1},{17,25},{25,17},{2,10},{10... | collective-permute-start | bytes 565256 | tf_op jit(solution)/shard_map/ppermute | solution.py:541
  4.9 2.6 %collective-permute-start.3 = (f32[46,8,128]{2,1,0:T(8,128)S(1)}, f32[46,8,128]{2,1,0:T(8,128)S(1)}, u32[]{:S(2)}, u32[]{:S(2)}) collective-permute-start(f32[46,8,128]{2,1,0:T(8,128)S(1)} %get-tuple-element.25), channel_id=1, source_target_pairs={{0,24},{8,16},{16,8},{24,0},{1,25},{9,17},{17,9},{25,1},{2,26},{10... | collective-permute-start | bytes 565256 | tf_op jit(solution)/shard_map/ppermute | solution.py:538
  7.5 1.5 %collective-permute-start = (f32[7,8,128]{2,1,0:T(8,128)S(1)}, f32[7,8,128]{2,1,0:T(8,128)S(1)}, u32[]{:S(2)}, u32[]{:S(2)}) collective-permute-start(f32[7,8,128]{2,1,0:T(8,128)S(1)} %get-tuple-element.17), channel_id=1, source_target_pairs={{0,1},{1,2},{2,3},{3,4},{4,5},{5,6},{6,7},{7,0},{8,9},{9,10},{10,1... | collective-permute-start | bytes 86024 | tf_op jit(solution)/shard_map/ppermute | solution.py:539
  9.0 3.2 %collective-permute-start.1 = (f32[7,8,128]{2,1,0:T(8,128)S(1)}, f32[7,8,128]{2,1,0:T(8,128)S(1)}, u32[]{:S(2)}, u32[]{:S(2)}) collective-permute-start(f32[7,8,128]{2,1,0:T(8,128)S(1)} %get-tuple-element.18), channel_id=1, source_target_pairs={{1,0},{2,1},{3,2},{4,3},{5,4},{6,5},{7,6},{0,7},{9,8},{10,9},{11,1... | collective-permute-start | bytes 86024 | tf_op jit(solution)/shard_map/ppermute | solution.py:540
  12.3 1.8 %collective-permute-done.from_low = f32[7,8,128]{2,1,0:T(8,128)S(1)} collective-permute-done((f32[7,8,128]{2,1,0:T(8,128)S(1)}, f32[7,8,128]{2,1,0:T(8,128)S(1)}, u32[]{:S(2)}, u32[]{:S(2)}) %collective-permute-start) | collective-permute-done | bytes 28704 | tf_op jit(solution)/shard_map/ppermute | solution.py:539
  14.1 0.0 collective-permute-done.1.from_high
  14.1 0.0 copy-start.1
  14.1 0.0 copy-start.2
  14.1 0.2 edges.1
  14.3 0.1 collective-permute-start.4
  14.4 0.4 %collective-permute-start.5 = (f32[7,8,128]{2,1,0:T(8,128)S(1)}, f32[7,8,128]{2,1,0:T(8,128)S(1)}, u32[]{:S(2)}, u32[]{:S(2)}) collective-permute-start(f32[7,8,128]{2,1,0:T(8,128)S(1)} %get-tuple-element.27), channel_id=1, source_target_pairs={{0,24},{8,16},{16,8},{24,0},{1,25},{9,17},{17,9},{25,1},{2,26},{10... | collective-permute-start | bytes 86024 | tf_op jit(solution)/shard_map/ppermute | solution.py:550
  14.8 0.0 copy-done
  14.8 0.2 copy-done.1
  15.0 0.0 copy-done.2
  15.0 2.4 %inner_rows.1 = (f32[8,16,8,128]{3,2,1,0:T(8,128)S(1)}, f32[16,8,128]{2,1,0:T(8,128)S(1)}, f32[2,4,8,8,128]{4,3,2,1,0:T(8,128)S(1)}) custom-call(f32[8,128,128]{2,1,0:T(8,128)S(1)} %bitcast.8, f32[128,128]{1,0:T(8,128)S(1)} %bitcast.13, f32[128,128]{1,0:T(8,128)S(1)} %bitcast.10, f32[12,3,8,128]{3,2,1,0:T(8,128)S(1)} %get-tuple-element.19.joined, ...), custom_call_target="tpu_custom_call" | custom-call | flops 40000000 | bytes 2000000 | tf_op jit(solution)/shard_map/inner_rows/pallas_call | solution.py:551
  17.3 0.0 collective-permute-done.4.corner0
  17.4 0.4 %collective-permute-done.5.corner1 = f32[7,8,128]{2,1,0:T(8,128)S(1)} collective-permute-done((f32[7,8,128]{2,1,0:T(8,128)S(1)}, f32[7,8,128]{2,1,0:T(8,128)S(1)}, u32[]{:S(2)}, u32[]{:S(2)}) %collective-permute-start.5) | collective-permute-done | bytes 28704 | tf_op jit(solution)/shard_map/ppermute | solution.py:550
  17.7 0.0 collective-permute-done.2.from0
  17.7 0.0 collective-permute-done.3.from1
  17.7 2.9 %outer_rows.1 = (f32[8,128,128]{2,1,0:T(8,128)}, f32[128,128]{1,0:T(8,128)}) custom-call(f32[8,16,8,128]{3,2,1,0:T(8,128)S(1)} %get-tuple-element.21.u_mid, f32[16,8,128]{2,1,0:T(8,128)S(1)} %get-tuple-element.22.ion_mid, f32[2,4,8,8,128]{4,3,2,1,0:T(8,128)S(1)} %get-tuple-element.23.saved, f32[128,128]{1,0:T(8,128)S(1)} %bitcast.11, ...), custom_call_target="tpu_custom_call" | custom-call | tf_op jit(solution)/shard_map/outer_rows/pallas_call | solution.py:566
Async XLA Ops:
  0.6 14.2 %copy-start = (f32[2,4,8,16,128]{4,3,2,1,0:T(8,128)S(1)}, f32[2,4,8,16,128]{4,3,2,1,0:T(8,128)}, u32[]{:S(2)}) copy-start(f32[2,4,8,16,128]{4,3,2,1,0:T(8,128)} %param.7) | copy-start | bytes 1572868
  4.4 13.4 %collective-permute-start.2 = (f32[46,8,128]{2,1,0:T(8,128)S(1)}, f32[46,8,128]{2,1,0:T(8,128)S(1)}, u32[]{:S(2)}, u32[]{:S(2)}) collective-permute-start(f32[46,8,128]{2,1,0:T(8,128)S(1)} %get-tuple-element.24), channel_id=1, source_target_pairs={{0,8},{8,0},{16,24},{24,16},{1,9},{9,1},{17,25},{25,17},{2,10},{10... | collective-permute-start | bytes 565256 | tf_op jit(solution)/shard_map/ppermute | solution.py:541
  4.9 12.8 %collective-permute-start.3 = (f32[46,8,128]{2,1,0:T(8,128)S(1)}, f32[46,8,128]{2,1,0:T(8,128)S(1)}, u32[]{:S(2)}, u32[]{:S(2)}) collective-permute-start(f32[46,8,128]{2,1,0:T(8,128)S(1)} %get-tuple-element.25), channel_id=1, source_target_pairs={{0,24},{8,16},{16,8},{24,0},{1,25},{9,17},{17,9},{25,1},{2,26},{10... | collective-permute-start | bytes 565256 | tf_op jit(solution)/shard_map/ppermute | solution.py:538
  7.5 6.6 %collective-permute-start = (f32[7,8,128]{2,1,0:T(8,128)S(1)}, f32[7,8,128]{2,1,0:T(8,128)S(1)}, u32[]{:S(2)}, u32[]{:S(2)}) collective-permute-start(f32[7,8,128]{2,1,0:T(8,128)S(1)} %get-tuple-element.17), channel_id=1, source_target_pairs={{0,1},{1,2},{2,3},{3,4},{4,5},{5,6},{6,7},{7,0},{8,9},{9,10},{10,1... | collective-permute-start | bytes 86024 | tf_op jit(solution)/shard_map/ppermute | solution.py:539
  9.0 5.1 %collective-permute-start.1 = (f32[7,8,128]{2,1,0:T(8,128)S(1)}, f32[7,8,128]{2,1,0:T(8,128)S(1)}, u32[]{:S(2)}, u32[]{:S(2)}) collective-permute-start(f32[7,8,128]{2,1,0:T(8,128)S(1)} %get-tuple-element.18), channel_id=1, source_target_pairs={{1,0},{2,1},{3,2},{4,3},{5,4},{6,5},{7,6},{0,7},{9,8},{10,9},{11,1... | collective-permute-start | bytes 86024 | tf_op jit(solution)/shard_map/ppermute | solution.py:540
  14.1 0.8 %copy-start.1 = (f32[8,16,128]{2,1,0:T(8,128)S(1)}, f32[8,16,128]{2,1,0:T(8,128)}, u32[]{:S(2)}) copy-start(f32[8,16,128]{2,1,0:T(8,128)} %param.9) | copy-start | bytes 196612
  14.1 0.9 %copy-start.2 = (f32[8,16,128]{2,1,0:T(8,128)S(1)}, f32[8,16,128]{2,1,0:T(8,128)}, u32[]{:S(2)}) copy-start(f32[8,16,128]{2,1,0:T(8,128)} %param.8) | copy-start | bytes 196612
  14.3 3.1 %collective-permute-start.4 = (f32[7,8,128]{2,1,0:T(8,128)S(1)}, f32[7,8,128]{2,1,0:T(8,128)S(1)}, u32[]{:S(2)}, u32[]{:S(2)}) collective-permute-start(f32[7,8,128]{2,1,0:T(8,128)S(1)} %get-tuple-element.26), channel_id=1, source_target_pairs={{0,8},{8,0},{16,24},{24,16},{1,9},{9,1},{17,25},{25,17},{2,10},{10... | collective-permute-start | bytes 86024 | tf_op jit(solution)/shard_map/ppermute | solution.py:549
  14.4 3.4 %collective-permute-start.5 = (f32[7,8,128]{2,1,0:T(8,128)S(1)}, f32[7,8,128]{2,1,0:T(8,128)S(1)}, u32[]{:S(2)}, u32[]{:S(2)}) collective-permute-start(f32[7,8,128]{2,1,0:T(8,128)S(1)} %get-tuple-element.27), channel_id=1, source_target_pairs={{0,24},{8,16},{16,8},{24,0},{1,25},{9,17},{17,9},{25,1},{2,26},{10... | collective-permute-start | bytes 86024 | tf_op jit(solution)/shard_map/ppermute | solution.py:550
